TPU v7x, 256 devices: a whole 4x4x8 slice. The times are simulated.
256 devices in a mesh: row: 16 (over x, y), col: 16 (over z, core).
Axes of the slice: x: 4, y: 4, z: 8, core: 2. Of those that a mesh axis runs over, the one named last changes fastest.
Arguments:
- tiles: bfloat16 [16, 16, 128, 128, 128], P('row', 'col'), may hold values from 0 to 0.31
- block_rows: int32 [16, 16, 128], P('row', 'col'), may hold values from 0 to 255, as said below
- block_cols: int32 [16, 16, 128], P('row', 'col'), may hold values from 0 to 255
- counts: int32 [16, 16], P('row', 'col'), may hold values from 1 to 128, as said below
- seeds: int32 [8, 524288], P(None, ('col', 'row')), may hold values from 1 to 999
Outputs:
- vectors_out: float32 [8, 524288], P(None, ('col', 'row'))
- deltas: float32 [4, 8], replicated
Inputs may be any that keep to these rules, and one draw needn't show every extreme that they name: `counts`: each entry is 1, a half, a quarter or an eighth of 128 (at least 1); some device is full in every draw. On each device, among the values of block_rows (over all 128 slots) that share one quotient by 16, at most 4 are distinct; on a device whose count is 128, some quotient has exactly 4 distinct values among its tiles.
All inputs are finite; a program needn't handle non-finite values.
Results may differ from a plain program's by a relative error of at most 0.00061.
Values may be sent and summed in bfloat16 or wider, within the bound.
A program may use at most 64 MiB of HBM per device.

v0:
```python
import functools

import jax
import jax.numpy as jnp
from jax import lax
from jax.sharding import Mesh
from jax.sharding import PartitionSpec as P

BLOCK = 128
TILE_BLOCK = 32
ITERS = 4
ROW_CAP = 4
ROW = ("row_0", "row_1")
COL = ("col_0", "col_1")
ROW_COL = ("row_0", "row_1", "col_0", "col_1")
COL_ROW = ("col_0", "col_1", "row_0", "row_1")


def by_axis(value, axes):
    return functools.reduce(lax.psum, axes, value)


def in_one_piece(arrays, axis, split_dim, concat_dim, along):
    ends, at = ([], 0)
    for a in arrays[:-1]:
        at += a.shape[along]
        ends.append(at)
    both = jnp.concatenate(arrays, axis=along)
    return tuple(
        jnp.split(
            lax.all_to_all(both, axis, split_axis=split_dim, concat_axis=concat_dim, tiled=True),
            ends,
            axis=along,
        )
    )


def over_axes(value, axes):
    return functools.reduce(lax.pmax, axes, value)


def apply_tiles(partial_value, gathered, panel_block, target_block, cols_block, weight):
    taken_rows = gathered[cols_block]
    product = jnp.einsum(
        "tkc,trc->tkr", taken_rows, panel_block, preferred_element_type=jnp.float32
    )
    return partial_value.at[target_block].add(product * weight[:, None, None])


def on_device(tiles, block_rows, block_cols, counts, seeds):
    panels = tiles[0, 0]
    rows_local = block_rows[0, 0]
    cols_local = block_cols[0, 0]
    count_here = counts[0, 0]
    vectors = seeds.shape[0]
    piece_len = seeds.shape[1]
    piece_blocks = piece_len // BLOCK
    row_count = lax.axis_size(ROW)
    total_nodes = piece_len * row_count * lax.axis_size(COL)
    row_span = row_count * piece_blocks
    tile_total = panels.shape[0]
    lane_index = jnp.arange(TILE_BLOCK, dtype=jnp.int32)
    tile_index = jnp.arange(tile_total, dtype=jnp.int32)
    live_flag = tile_index < count_here
    live_mask = live_flag.astype(jnp.float32)
    block_index = jnp.arange(row_span, dtype=jnp.int32)
    hits = (rows_local[None, :] == block_index[:, None]) & live_flag[None, :]
    present = jnp.max(hits.astype(jnp.int32), axis=1).reshape(row_count, piece_blocks)
    rank = jnp.cumsum(present, axis=1) - present
    owner_index = jnp.arange(row_count, dtype=jnp.int32)
    block_slot = (owner_index[:, None] * ROW_CAP + rank).reshape(row_span)
    slot_total = row_count * ROW_CAP
    matched = jnp.where(rows_local[:, None] == block_index[None, :], block_slot[None, :], 0)
    targets = jnp.minimum(jnp.sum(matched, axis=1), slot_total - 1)
    slot_index = jnp.arange(ROW_CAP, dtype=jnp.int32)
    offset_index = jnp.arange(piece_blocks, dtype=jnp.int32)
    matches = (present[:, None, :] == 1) & (rank[:, None, :] == slot_index[None, :, None])
    slot_ids = jnp.sum(jnp.where(matches, offset_index[None, None, :], 0), axis=2)
    row_total = jnp.sum(panels, axis=2, dtype=jnp.float32) * live_mask[:, None]
    degree_part = (
        jnp.zeros((slot_total, 1, BLOCK), jnp.float32).at[targets].add(row_total[:, None, :])
    )
    seed_float = seeds.astype(jnp.float32)
    seed_total = by_axis(jnp.sum(seed_float, axis=1), ROW_COL)
    current = (
        (total_nodes * seed_float / seed_total[:, None])
        .reshape(vectors, piece_blocks, BLOCK)
        .transpose(1, 0, 2)
    )
    empty_sum = jnp.zeros((slot_total, vectors, BLOCK), jnp.float32)
    deltas = []
    divisor = None
    owner_table = None
    for iteration in range(ITERS):
        current_half = current.astype(jnp.bfloat16)
        gathered = lax.all_gather(current_half, COL, axis=0, tiled=True)

        def advance(block_at, partial_value):
            begin_at = block_at * TILE_BLOCK
            weight = (begin_at + lane_index < count_here).astype(jnp.float32)
            return apply_tiles(
                partial_value,
                gathered,
                lax.dynamic_slice_in_dim(panels, begin_at, TILE_BLOCK, 0),
                lax.dynamic_slice_in_dim(targets, begin_at, TILE_BLOCK, 0),
                lax.dynamic_slice_in_dim(cols_local, begin_at, TILE_BLOCK, 0),
                weight,
            )

        partial_value = lax.fori_loop(
            0, (count_here + TILE_BLOCK - 1) // TILE_BLOCK, advance, empty_sum
        )
        shaped = partial_value.reshape(row_count, ROW_CAP, vectors, BLOCK)
        if iteration == 0:
            degree_shaped = degree_part.reshape(row_count, ROW_CAP, 1, BLOCK)
            incoming, degree_in, received_ids = (
                *in_one_piece((shaped, degree_shaped), ROW, 0, 0, 2),
                lax.all_to_all(slot_ids, ROW, split_axis=0, concat_axis=0, tiled=True),
            )
            block_index_own = jnp.arange(piece_blocks, dtype=jnp.int32)
            owner_table = (received_ids.reshape(-1)[None, :] == block_index_own[:, None]).astype(
                jnp.float32
            )
            degree_piece = jnp.dot(
                owner_table,
                degree_in.reshape(row_count * ROW_CAP, BLOCK),
                precision=lax.Precision.HIGHEST,
                preferred_element_type=jnp.float32,
            )
            divisor = 1.0 + degree_piece.reshape(piece_blocks, 1, BLOCK)
        else:
            incoming = lax.all_to_all(shaped, ROW, split_axis=0, concat_axis=0, tiled=True)
        summed = jnp.dot(
            owner_table,
            incoming.reshape(row_count * ROW_CAP, vectors * BLOCK),
            precision=lax.Precision.HIGHEST,
            preferred_element_type=jnp.float32,
        ).reshape(piece_blocks, vectors, BLOCK)
        raw_next = (summed + current) / divisor
        local_total = jnp.sum(raw_next, axis=(0, 2))
        totals = by_axis(local_total, ROW_COL)
        updated = total_nodes * raw_next / totals[None, :, None]
        deltas.append(over_axes(jnp.max(jnp.abs(updated - current), axis=(0, 2)), ROW_COL))
        current = updated
    vectors_out = current.transpose(1, 0, 2).reshape(vectors, piece_len)
    return (vectors_out, jnp.stack(deltas))


def solution(mesh):
    torus = Mesh(mesh.devices.reshape(4, 4, 8, 2), ("row_0", "row_1", "col_0", "col_1"))
    in_specs = (
        P(ROW, COL, None, None, None),
        P(ROW, COL, None),
        P(ROW, COL, None),
        P(ROW, COL),
        P(None, COL_ROW),
    )
    out_specs = (P(None, COL_ROW), P())
    return jax.shard_map(
        on_device, mesh=torus, in_specs=in_specs, out_specs=out_specs, check_vma=False
    )
```

profile of v0, /device:TPU:1, one launch (start us, length us, event | category | flops | bytes accessed | tf_op | source)
XLA Modules:
  0.0 434.4 jit_solution(14772256052464649446)
XLA Ops:
  1.3 0.8 convert_reduce_fusion.1
  2.5 0.7 copy.41
  3.2 7.6 %all-to-all-start = ((s32[16,1,4]{2,1,0:T(1,128)}), s32[16,1,4]{2,1,0:T(1,128)S(1)}, u32[]{:S(2)}, u32[]{:S(2)}) async-start(s32[16,1,4]{2,1,0:T(1,128)} %copy.41), calls=%async_computation | async-start | bytes 16384 | tf_op jit(solution)/shard_map/all_to_all | solution.py:118
  11.0 0.8 select_reduce_fusion
  11.9 1.0 convert_reduce_fusion.2
  12.9 8.6 %psum.140 = f32[8]{0:T(128)S(1)} all-reduce(f32[8]{0:T(128)S(1)} %convert_reduce_fusion.2), channel_id=1, replica_groups=mesh['row_0'=4,'row_1'=4,'col_0'=8,'col_1'=2] {'row_0'}, use_global_device_ids=true, to_apply=%region_5.6 | all-reduce | flops 8 | bytes 64 | tf_op jit(solution)/shard_map/psum | solution.py:20
  21.4 8.4 %psum.141 = f32[8]{0:T(128)S(1)} all-reduce(f32[8]{0:T(128)S(1)} %psum.140), channel_id=1, replica_groups=mesh['row_0'=4,'row_1'=4,'col_0'=8,'col_1'=2] {'row_1'}, use_global_device_ids=true, to_apply=%region_6.7 | all-reduce | flops 8 | bytes 64 | tf_op jit(solution)/shard_map/psum | solution.py:20
  29.8 16.2 %psum.142 = f32[8]{0:T(128)S(1)} all-reduce(f32[8]{0:T(128)S(1)} %psum.141), channel_id=1, replica_groups=mesh['row_0'=4,'row_1'=4,'col_0'=8,'col_1'=2] {'col_0'}, use_global_device_ids=true, to_apply=%region_7.8 | all-reduce | flops 8 | bytes 64 | tf_op jit(solution)/shard_map/psum | solution.py:20
  46.0 11.1 %psum.143 = f32[8]{0:T(128)S(1)} all-reduce(f32[8]{0:T(128)S(1)} %psum.142), channel_id=1, replica_groups=mesh['row_0'=4,'row_1'=4,'col_0'=8,'col_1'=2] {'col_1'}, use_global_device_ids=true, to_apply=%region_8.9 | all-reduce | flops 8 | bytes 64 | tf_op jit(solution)/shard_map/psum | solution.py:20
  57.2 0.9 divide_bitcast_fusion.1
  58.1 15.9 %all_gather.12 = bf16[256,8,128]{2,0,1:T(8,128)(2,1)S(1)} all-gather(bf16[16,8,128]{2,0,1:T(8,128)(2,1)S(1)} %bitcast.220), channel_id=1, replica_groups=mesh['row_0'=4,'row_1'=4,'col_0'=8,'col_1'=2] {'col_0','col_1'}, dimensions={0}, use_global_device_ids=true | all-gather | bytes 557056 | tf_op jit(solution)/shard_map/all_gather | solution.py:96
  74.4 3.4 convert_reduce_fusion
  77.8 4.9 %while.44 = (s32[]{:T(128)}, f32[64,8,128]{2,1,0:T(8,128)S(1)}, s32[]{:T(128)}, s32[128]{0:T(128)S(1)}, s32[128]{0:T(128)S(1)}, /*index=5*/bf16[256,8,128]{2,1,0...) while((s32[]{:T(128)}, f32[64,8,128]{2,1,0:T(8,128)S(1)}, ...), condition=%wide.region_11.12_spmd.clone, body=%wide.region_9.11_spmd.clone.sunk | while | flops 8455462 | bytes 1774899 | solution.py:110
  77.9 0.6 gather_fusion
  78.5 0.6 compare_convert_fusion.8
  79.2 1.9 convolution_multiply_fusion.8
  81.0 1.7 scatter_fusion
  82.7 1.1 scatter_custom_fusion.4
  83.9 0.8 copy.43
  84.7 15.8 %all-to-all-start.1 = ((f32[16,4,9,128]{3,1,2,0:T(4,128)}), f32[16,4,9,128]{3,1,2,0:T(4,128)S(1)}, u32[]{:S(2)}, u32[]{:S(2)}) async-start(f32[16,4,9,128]{3,1,2,0:T(4,128)} %copy.43), calls=%async_computation.1 | async-start | bytes 589824 | tf_op jit(solution)/shard_map/all_to_all | solution.py:31
  101.0 0.7 reduce.3
  101.8 6.2 %all-to-all-done.1 = f32[16,4,9,128]{3,1,2,0:T(4,128)S(1)} async-done(((f32[16,4,9,128]{3,1,2,0:T(4,128)}), f32[16,4,9,128]{3,1,2,0:T(4,128)S(1)}, u32[]{:S(2)}, u32[]{:S(2)}) %all-to-all-start.1) | async-done | bytes 294944 | tf_op jit(solution)/shard_map/all_to_all | solution.py:31
  108.6 7.0 %psum.144 = f32[8]{0:T(128)S(1)} all-reduce(f32[8]{0:T(128)S(1)} %get-tuple-element.534), channel_id=1, replica_groups=mesh['row_0'=4,'row_1'=4,'col_0'=8,'col_1'=2] {'row_0'}, use_global_device_ids=true, to_apply=%region_15.16 | all-reduce | flops 8 | bytes 64 | tf_op jit(solution)/shard_map/psum | solution.py:20
  115.6 6.4 %psum.145 = f32[8]{0:T(128)S(1)} all-reduce(f32[8]{0:T(128)S(1)} %psum.144), channel_id=1, replica_groups=mesh['row_0'=4,'row_1'=4,'col_0'=8,'col_1'=2] {'row_1'}, use_global_device_ids=true, to_apply=%region_16.17 | all-reduce | flops 8 | bytes 64 | tf_op jit(solution)/shard_map/psum | solution.py:20
  122.0 14.7 %psum.146 = f32[8]{0:T(128)S(1)} all-reduce(f32[8]{0:T(128)S(1)} %psum.145), channel_id=1, replica_groups=mesh['row_0'=4,'row_1'=4,'col_0'=8,'col_1'=2] {'col_0'}, use_global_device_ids=true, to_apply=%region_17.18 | all-reduce | flops 8 | bytes 64 | tf_op jit(solution)/shard_map/psum | solution.py:20
  136.7 10.4 %psum.147 = f32[8]{0:T(128)S(1)} all-reduce(f32[8]{0:T(128)S(1)} %psum.146), channel_id=1, replica_groups=mesh['row_0'=4,'row_1'=4,'col_0'=8,'col_1'=2] {'col_1'}, use_global_device_ids=true, to_apply=%region_18.19 | all-reduce | flops 8 | bytes 64 | tf_op jit(solution)/shard_map/psum | solution.py:20
  147.2 15.9 %all_gather.13 = bf16[256,8,128]{2,0,1:T(8,128)(2,1)S(1)} all-gather(bf16[16,8,128]{2,0,1:T(8,128)(2,1)S(1)} %get-tuple-element.524), channel_id=1, replica_groups=mesh['row_0'=4,'row_1'=4,'col_0'=8,'col_1'=2] {'col_0','col_1'}, dimensions={0}, use_global_device_ids=true | all-gather | bytes 557056 | tf_op jit(solution)/shard_map/all_gather | solution.py:96
  163.5 4.9 %while.45 = (s32[]{:T(128)}, f32[64,8,128]{2,1,0:T(8,128)S(1)}, s32[]{:T(128)}, s32[128]{0:T(128)S(1)}, s32[128]{0:T(128)S(1)}, /*index=5*/bf16[256,8,128]{2,1,0...) while((s32[]{:T(128)}, f32[64,8,128]{2,1,0:T(8,128)S(1)}, ...), condition=%wide.region_21.22_spmd.clone, body=%wide.region_19.21_spmd.clone.sunk | while | flops 8455462 | bytes 1774899 | solution.py:110
  163.6 0.6 gather_fusion.1
  164.2 0.6 compare_convert_fusion.9
  164.9 1.9 convolution_multiply_fusion.9
  166.7 1.7 scatter_fusion.1
  168.4 25.1 %all_to_all.29 = f32[16,4,8,128]{3,2,1,0:T(8,128)S(1)} all-to-all(f32[16,4,8,128]{3,2,1,0:T(8,128)S(1)} %bitcast.212), channel_id=1, replica_groups=mesh['row_0'=4,'row_1'=4,'col_0'=8,'col_1'=2] {'row_0','row_1'}, dimensions={0} | all-to-all | bytes 524288 | tf_op jit(solution)/shard_map/all_to_all | solution.py:132
  193.9 7.5 %psum.148 = f32[8]{0:T(128)S(1)} all-reduce(f32[8]{0:T(128)S(1)} %get-tuple-element.435), channel_id=1, replica_groups=mesh['row_0'=4,'row_1'=4,'col_0'=8,'col_1'=2] {'row_0'}, use_global_device_ids=true, to_apply=%region_23.24 | all-reduce | flops 8 | bytes 64 | tf_op jit(solution)/shard_map/psum | solution.py:20
  201.3 6.0 %psum.149 = f32[8]{0:T(128)S(1)} all-reduce(f32[8]{0:T(128)S(1)} %psum.148), channel_id=1, replica_groups=mesh['row_0'=4,'row_1'=4,'col_0'=8,'col_1'=2] {'row_1'}, use_global_device_ids=true, to_apply=%region_24.25 | all-reduce | flops 8 | bytes 64 | tf_op jit(solution)/shard_map/psum | solution.py:20
  207.4 12.3 %psum.150 = f32[8]{0:T(128)S(1)} all-reduce(f32[8]{0:T(128)S(1)} %psum.149), channel_id=1, replica_groups=mesh['row_0'=4,'row_1'=4,'col_0'=8,'col_1'=2] {'col_0'}, use_global_device_ids=true, to_apply=%region_25.26 | all-reduce | flops 8 | bytes 64 | tf_op jit(solution)/shard_map/psum | solution.py:20
  219.7 11.2 %psum.151 = f32[8]{0:T(128)S(1)} all-reduce(f32[8]{0:T(128)S(1)} %psum.150), channel_id=1, replica_groups=mesh['row_0'=4,'row_1'=4,'col_0'=8,'col_1'=2] {'col_1'}, use_global_device_ids=true, to_apply=%region_26.27 | all-reduce | flops 8 | bytes 64 | tf_op jit(solution)/shard_map/psum | solution.py:20
  231.0 15.9 %all_gather.14 = bf16[256,8,128]{2,0,1:T(8,128)(2,1)S(1)} all-gather(bf16[16,8,128]{2,0,1:T(8,128)(2,1)S(1)} %get-tuple-element.522), channel_id=1, replica_groups=mesh['row_0'=4,'row_1'=4,'col_0'=8,'col_1'=2] {'col_0','col_1'}, dimensions={0}, use_global_device_ids=true | all-gather | bytes 557056 | tf_op jit(solution)/shard_map/all_gather | solution.py:96
  247.3 4.9 %while.46 = (s32[]{:T(128)}, f32[64,8,128]{2,1,0:T(8,128)S(1)}, s32[]{:T(128)}, s32[128]{0:T(128)S(1)}, s32[128]{0:T(128)S(1)}, /*index=5*/bf16[256,8,128]{2,1,0...) while((s32[]{:T(128)}, f32[64,8,128]{2,1,0:T(8,128)S(1)}, ...), condition=%wide.region_29.30_spmd.clone, body=%wide.region_27.29_spmd.clone.sunk | while | flops 8455462 | bytes 1774899 | solution.py:110
  247.4 0.6 gather_fusion.2
  248.0 0.6 compare_convert_fusion.10
  248.7 1.9 convolution_multiply_fusion.10
  250.6 1.7 scatter_fusion.2
  252.2 24.9 %all_to_all.30 = f32[16,4,8,128]{3,2,1,0:T(8,128)S(1)} all-to-all(f32[16,4,8,128]{3,2,1,0:T(8,128)S(1)} %bitcast.213), channel_id=1, replica_groups=mesh['row_0'=4,'row_1'=4,'col_0'=8,'col_1'=2] {'row_0','row_1'}, dimensions={0} | all-to-all | bytes 524288 | tf_op jit(solution)/shard_map/all_to_all | solution.py:132
  277.5 7.5 %psum.152 = f32[8]{0:T(128)S(1)} all-reduce(f32[8]{0:T(128)S(1)} %get-tuple-element.437), channel_id=1, replica_groups=mesh['row_0'=4,'row_1'=4,'col_0'=8,'col_1'=2] {'row_0'}, use_global_device_ids=true, to_apply=%region_31.32 | all-reduce | flops 8 | bytes 64 | tf_op jit(solution)/shard_map/psum | solution.py:20
  285.0 6.1 %psum.153 = f32[8]{0:T(128)S(1)} all-reduce(f32[8]{0:T(128)S(1)} %psum.152), channel_id=1, replica_groups=mesh['row_0'=4,'row_1'=4,'col_0'=8,'col_1'=2] {'row_1'}, use_global_device_ids=true, to_apply=%region_32.33 | all-reduce | flops 8 | bytes 64 | tf_op jit(solution)/shard_map/psum | solution.py:20
  291.1 12.4 %psum.154 = f32[8]{0:T(128)S(1)} all-reduce(f32[8]{0:T(128)S(1)} %psum.153), channel_id=1, replica_groups=mesh['row_0'=4,'row_1'=4,'col_0'=8,'col_1'=2] {'col_0'}, use_global_device_ids=true, to_apply=%region_33.34 | all-reduce | flops 8 | bytes 64 | tf_op jit(solution)/shard_map/psum | solution.py:20
  303.5 11.2 %psum.155 = f32[8]{0:T(128)S(1)} all-reduce(f32[8]{0:T(128)S(1)} %psum.154), channel_id=1, replica_groups=mesh['row_0'=4,'row_1'=4,'col_0'=8,'col_1'=2] {'col_1'}, use_global_device_ids=true, to_apply=%region_34.35 | all-reduce | flops 8 | bytes 64 | tf_op jit(solution)/shard_map/psum | solution.py:20
  314.8 15.9 %all_gather.15 = bf16[256,8,128]{2,0,1:T(8,128)(2,1)S(1)} all-gather(bf16[16,8,128]{2,0,1:T(8,128)(2,1)S(1)} %get-tuple-element.520), channel_id=1, replica_groups=mesh['row_0'=4,'row_1'=4,'col_0'=8,'col_1'=2] {'col_0','col_1'}, dimensions={0}, use_global_device_ids=true | all-gather | bytes 557056 | tf_op jit(solution)/shard_map/all_gather | solution.py:96
  331.1 4.9 %while.47 = (s32[]{:T(128)}, f32[64,8,128]{2,1,0:T(8,128)S(1)}, s32[]{:T(128)}, s32[128]{0:T(128)S(1)}, s32[128]{0:T(128)S(1)}, /*index=5*/bf16[256,8,128]{2,1,0...) while((s32[]{:T(128)}, f32[64,8,128]{2,1,0:T(8,128)S(1)}, ...), condition=%wide.region_37.38_spmd.clone, body=%wide.region_35.37_spmd.clone.sunk | while | flops 8455462 | bytes 1774899 | solution.py:110
  331.2 0.6 gather_fusion.3
  331.8 0.6 compare_convert_fusion.11
  332.4 1.9 convolution_multiply_fusion.11
  334.3 1.7 scatter_fusion.3
  336.0 24.9 %all_to_all.31 = f32[16,4,8,128]{3,2,1,0:T(8,128)S(1)} all-to-all(f32[16,4,8,128]{3,2,1,0:T(8,128)S(1)} %bitcast.211), channel_id=1, replica_groups=mesh['row_0'=4,'row_1'=4,'col_0'=8,'col_1'=2] {'row_0','row_1'}, dimensions={0} | all-to-all | bytes 524288 | tf_op jit(solution)/shard_map/all_to_all | solution.py:132
  361.3 7.5 %psum.156 = f32[8]{0:T(128)S(1)} all-reduce(f32[8]{0:T(128)S(1)} %get-tuple-element.538), channel_id=1, replica_groups=mesh['row_0'=4,'row_1'=4,'col_0'=8,'col_1'=2] {'row_0'}, use_global_device_ids=true, to_apply=%region_39.40 | all-reduce | flops 8 | bytes 64 | tf_op jit(solution)/shard_map/psum | solution.py:20
  368.7 6.1 %psum.157 = f32[8]{0:T(128)S(1)} all-reduce(f32[8]{0:T(128)S(1)} %psum.156), channel_id=1, replica_groups=mesh['row_0'=4,'row_1'=4,'col_0'=8,'col_1'=2] {'row_1'}, use_global_device_ids=true, to_apply=%region_40.41 | all-reduce | flops 8 | bytes 64 | tf_op jit(solution)/shard_map/psum | solution.py:20
  374.8 12.4 %psum.158 = f32[8]{0:T(128)S(1)} all-reduce(f32[8]{0:T(128)S(1)} %psum.157), channel_id=1, replica_groups=mesh['row_0'=4,'row_1'=4,'col_0'=8,'col_1'=2] {'col_0'}, use_global_device_ids=true, to_apply=%region_41.42 | all-reduce | flops 8 | bytes 64 | tf_op jit(solution)/shard_map/psum | solution.py:20
  387.2 11.2 %psum.159 = f32[8]{0:T(128)S(1)} all-reduce(f32[8]{0:T(128)S(1)} %psum.158), channel_id=1, replica_groups=mesh['row_0'=4,'row_1'=4,'col_0'=8,'col_1'=2] {'col_1'}, use_global_device_ids=true, to_apply=%region_42.43 | all-reduce | flops 8 | bytes 64 | tf_op jit(solution)/shard_map/psum | solution.py:20
  398.8 0.7 copy.108
  399.4 6.8 %all-reduce.2 = (f32[8]{0:T(128)S(1)}, f32[8]{0:T(128)S(1)}, f32[8]{0:T(128)S(1)}, f32[8]{0:T(128)S(1)}) all-reduce(f32[8]{0:T(128)S(1)} %get-tuple-element.439, f32[8]{0:T(128)S(1)} %get-tuple-element.438, f32[8]{0:T(128)S(1)} %get-tuple-element.436, ...), channel_id=1, replica_groups=mesh['row_0'=4,'row_1'=4,'col_0'=8,'col_1'=2] {'row_0'}, use_global_device_ids=true, to_apply=%region_59.60 | all-reduce | flops 32 | bytes 256 | tf_op jit(solution)/shard_map/pmax | solution.py:39
  406.2 6.8 %all-reduce.1 = (f32[8]{0:T(128)S(1)}, f32[8]{0:T(128)S(1)}, f32[8]{0:T(128)S(1)}, f32[8]{0:T(128)S(1)}) all-reduce(f32[8]{0:T(128)S(1)} %get-tuple-element.512, f32[8]{0:T(128)S(1)} %get-tuple-element.513, f32[8]{0:T(128)S(1)} %get-tuple-element.514, ...), channel_id=1, replica_groups=mesh['row_0'=4,'row_1'=4,'col_0'=8,'col_1'=2] {'row_1'}, use_global_device_ids=true, to_apply=%region_60.61 | all-reduce | flops 32 | bytes 256 | tf_op jit(solution)/shard_map/pmax | solution.py:39
  413.0 11.0 %all-reduce = (f32[8]{0:T(128)S(1)}, f32[8]{0:T(128)S(1)}, f32[8]{0:T(128)S(1)}, f32[8]{0:T(128)S(1)}) all-reduce(f32[8]{0:T(128)S(1)} %get-tuple-element.508, f32[8]{0:T(128)S(1)} %get-tuple-element.509, f32[8]{0:T(128)S(1)} %get-tuple-element.510, ...), channel_id=1, replica_groups=mesh['row_0'=4,'row_1'=4,'col_0'=8,'col_1'=2] {'col_0'}, use_global_device_ids=true, to_apply=%region_61.62 | all-reduce | flops 32 | bytes 256 | tf_op jit(solution)/shard_map/pmax | solution.py:39
  424.0 9.8 %all-reduce.3 = (f32[1,8]{1,0:T(1,128)S(1)}, f32[1,8]{1,0:T(1,128)S(1)}, f32[1,8]{1,0:T(1,128)S(1)}, f32[1,8]{1,0:T(1,128)S(1)}) all-reduce(f32[1,8]{1,0:T(1,128)S(1)} %bitcast.226, f32[1,8]{1,0:T(1,128)S(1)} %bitcast.227, f32[1,8]{1,0:T(1,128)S(1)} %bitcast.228, ...), channel_id=1, replica_groups=mesh['row_0'=4,'row_1'=4,'col_0'=8,'col_1'=2] {'col_1'}, use_global_device_ids=true, to_apply=%region_62.63 | all-reduce | flops 32 | bytes 256 | tf_op jit(solution)/shard_map/pmax | solution.py:39
  (50 shorter events, 5.9 us)
Async XLA Ops:
  0.6 77.2 %copy-start = (s32[1,1,128]{2,1,0:T(1,128)S(1)}, s32[1,1,128]{2,1,0:T(1,128)}, u32[]{:S(2)}) copy-start(s32[1,1,128]{2,1,0:T(1,128)} %param.15) | copy-start | bytes 1540
  3.2 81.5 %all-to-all-start = ((s32[16,1,4]{2,1,0:T(1,128)}), s32[16,1,4]{2,1,0:T(1,128)S(1)}, u32[]{:S(2)}, u32[]{:S(2)}) async-start(s32[16,1,4]{2,1,0:T(1,128)} %copy.41), calls=%async_computation | async-start | bytes 16384 | tf_op jit(solution)/shard_map/all_to_all | solution.py:118
  84.7 23.3 %all-to-all-start.1 = ((f32[16,4,9,128]{3,1,2,0:T(4,128)}), f32[16,4,9,128]{3,1,2,0:T(4,128)S(1)}, u32[]{:S(2)}, u32[]{:S(2)}) async-start(f32[16,4,9,128]{3,1,2,0:T(4,128)} %copy.43), calls=%async_computation.1 | async-start | bytes 589824 | tf_op jit(solution)/shard_map/all_to_all | solution.py:31
where the time goes:
time: 436 us; the launch traced here: 434 us
  blocking collectives  367 us (84%)
  starting transfers between devices  23.4 us (5%)
  other arithmetic  19.8 us (5%)
  matrix products  9.01 us (2%)
  local copies, waits for them, and re-layouts  6.96 us (2%)
  waiting for transfers between devices  6.24 us (1%)
    psum x20, blocking collectives, by_axis(): return functools.reduce(lax.psum, axes, value)  194 us
    all_to_all x3, blocking collectives, on_device(): lax.all_to_all(shaped, ROW, split_axis=0, concat_axis=0, tiled=True)  75 us
    all_gather x4, blocking collectives, on_device(): gathered = lax.all_gather(current_half, COL, axis=0, tiled=True)  63.6 us
    pmax x4, blocking collectives, over_axes(): return functools.reduce(lax.pmax, axes, value)  34.4 us
    all_to_all x1, starting transfers between devices, in_one_piece(): lax.all_to_all(both, axis, split_axis=split_dim, concat_axis=concat_dim,...  15.8 us
  transfers between devices with their start and end apart: 2, of which 1 were waited for; matrix products, arithmetic and copies ran while one was open for 3% of the time, Pallas kernels for 0%

commit v1 on v0

v1 whole, which is shorter than its diff:
```python
import functools

import jax
import jax.numpy as jnp
from jax import lax
from jax.experimental import pallas as pl
from jax.experimental.pallas import tpu as pltpu
from jax.sharding import PartitionSpec as P

BLOCK = 128
ITERS = 4
ROW_CAP = 4
K = 8
UNROLL = 16
DEAD = 1024
NT = (((1,), (1,)), ((), ()))
F32 = jnp.float32


def within(index, most):
    return jnp.minimum(jnp.maximum(index, 0), most)


def ring(delta, size):
    return min(delta % size, -delta % size)


def kernel(
    nx, ny, nz, pb, nodes,
    tiles_ref, rows_ref, cols_ref, counts_ref, seeds_ref,
    out_ref, deltas_ref,
    a_buf, g_even, g_odd, y_buf, p_buf, inc_even, inc_odd, v_buf, raw_buf, deg_buf,
    tab_v, tab_s, rank_v, ctab_v, ctab_s, ar_a, ar_b, st_a, st_b,
    a_sem, tab_sem, gr_sem, gs_sem, er_sem, es_sem, cr_sem, cs_sem, ra_sem, sa_sem, rb_sem, sb_sem,
):
    n_row, n_col = nx * ny, nz * 2
    g_buf, inc_buf = (g_even, g_odd), (inc_even, inc_odd)
    tile_total = a_buf.shape[0]
    slots = n_row * ROW_CAP
    i = lax.axis_index("row")
    j = lax.axis_index("col")
    px, py = i // ny, i % ny
    z, c = j // 2, j % 2
    other = z * 2 + (1 - c)

    row_offsets = sorted(
        [(dx, dy) for dx in range(nx) for dy in range(ny) if (dx, dy) != (0, 0)],
        key=lambda d: -(ring(d[0], nx) + ring(d[1], ny)),
    )
    z_offsets = sorted(range(1, nz), key=lambda d: -ring(d, nz))

    def row_peer(d):
        return lax.rem(px + d[0], nx) * ny + lax.rem(py + d[1], ny)

    def col_of(dz):
        return lax.rem(z + dz, nz) * 2 + c

    load = pltpu.make_async_copy(tiles_ref.at[0, 0], a_buf, a_sem)
    load.start()

    barrier = pltpu.get_barrier_semaphore()
    for d in row_offsets:
        pl.semaphore_signal(barrier, inc=1, device_id={"row": row_peer(d)})
    for o in range(1, n_col):
        pl.semaphore_signal(barrier, inc=1, device_id={"col": lax.rem(j + o, n_col)})

    I32 = jnp.int32
    sub = lax.broadcasted_iota(I32, (tile_total, 128), 0)
    lane = lax.broadcasted_iota(I32, (tile_total, 128), 1)
    count = counts_ref[0, 0]
    lane_row = lax.broadcasted_iota(I32, (1, 128), 1)
    key_r = jnp.where(lane_row < count, rows_ref[0], DEAD)
    key_rr = jnp.broadcast_to(key_r, (tile_total, 128))
    cols_rr = jnp.broadcast_to(cols_ref[0], (tile_total, 128))

    def lanes(value):
        return jnp.sum(value, axis=1, keepdims=True)

    def subs(value):
        return jnp.sum(value, axis=0, keepdims=True)

    def pick_if(mask, value):
        return jnp.where(mask, value, 0)

    key_c = lanes(pick_if(sub == lane, key_rr))
    cols_c = lanes(pick_if(sub == lane, cols_rr))
    key_cc = jnp.broadcast_to(key_c, (tile_total, 128))
    same = key_rr == key_cc
    before = lanes(pick_if(same & (lane < sub), 1))
    pos_c = before + lanes(pick_if(key_rr < key_cc, 1))
    last_c = lanes(pick_if(key_rr <= key_cc, 1)) - 1
    first_c = pick_if((before == 0) & (key_c < DEAD), 1)
    before_r = subs(pick_if(same & (sub < lane), 1))
    first_r = pick_if((before_r == 0) & (key_r < DEAD), 1)
    shift = pb.bit_length() - 1
    owner_c = key_c >> shift
    owner_r = key_r >> shift
    rank_c = lanes(
        pick_if((owner_r == owner_c) & (key_rr < key_cc), jnp.broadcast_to(first_r, sub.shape))
    )
    order = pos_c == lane
    perm_r = subs(pick_if(order, sub))
    cols_sorted = subs(pick_if(order, cols_c))
    keep_r = subs(pick_if(order, 1 - first_c))
    slot_c = owner_c * ROW_CAP + rank_c
    chosen = slot_c == lane
    end_r = subs(pick_if(chosen, first_c * last_c)) + (1 - subs(pick_if(chosen, first_c))) * tile_total
    tab_v[0] = perm_r
    tab_v[1] = cols_sorted
    tab_v[2] = keep_r
    tab_v[3] = end_r
    halves = rank_v.shape[0]
    per_half = 128 // pb
    for h in range(halves):
        found = subs(pick_if(key_c == lane + 128 * h, first_c * (rank_c + 1)))
        rank_v[h] = jnp.where(found > 0, found - 1 + i * ROW_CAP, slots)
    table = pltpu.make_async_copy(tab_v, tab_s, tab_sem)
    table.start()

    y_buf[tile_total] = jnp.zeros((K, BLOCK), F32)
    for par in range(2):
        inc_buf[par][slots] = jnp.zeros((K, BLOCK), F32)
    g_odd[...] = jnp.ones(g_odd.shape, jnp.bfloat16)

    seed_sum = jnp.zeros((K, BLOCK), F32)
    for b in range(pb):
        seed_sum += seeds_ref[:, b * BLOCK : (b + 1) * BLOCK].astype(F32)

    table.wait()
    load.wait()

    def products(par):
        def step(at, acc):
            for u in range(UNROLL):
                t = at * UNROLL + u
                x = g_buf[par][within(tab_s[1, 0, t], n_col * pb - 1)]
                a = a_buf[within(tab_s[0, 0, t], tile_total - 1)]
                y = lax.dot_general(x, a, NT, preferred_element_type=F32)
                acc = acc * tab_s[2, 0, t].astype(F32) + y
                y_buf[t] = acc
            return acc

        lax.fori_loop(0, tile_total // UNROLL, step, jnp.zeros((K, BLOCK), F32))

        def pick(at, carry):
            for u in range(8):
                q = at * 8 + u
                p_buf[par, q] = y_buf[within(tab_s[3, 0, q], tile_total)]
            return carry

        lax.fori_loop(0, slots // 8, pick, 0)

    def exchange_copy(par, d):
        o = row_peer(d)
        index = d[0] * ny + d[1]
        return pltpu.make_async_remote_copy(
            src_ref=p_buf.at[par, pl.ds(o * ROW_CAP, ROW_CAP)],
            dst_ref=inc_buf[par].at[pl.ds(i * ROW_CAP, ROW_CAP)],
            send_sem=es_sem.at[par, index],
            recv_sem=er_sem.at[par, index],
            device_id={"row": o},
        )

    def exchange_start(par):
        for d in row_offsets:
            exchange_copy(par, d).start()
        inc_buf[par][pl.ds(i * ROW_CAP, ROW_CAP)] = p_buf[par, pl.ds(i * ROW_CAP, ROW_CAP)]

    def exchange_wait(par):
        for d in reversed(row_offsets):
            exchange_copy(par, d).wait_recv()

    def exchange_done(par):
        for d in row_offsets:
            exchange_copy(par, d).wait_send()

    def rank_copy(d):
        o = row_peer(d)
        index = d[0] * ny + d[1]
        return pltpu.make_async_remote_copy(
            src_ref=rank_v.at[o // per_half],
            dst_ref=ctab_v.at[i],
            send_sem=cs_sem.at[index],
            recv_sem=cr_sem.at[index],
            device_id={"row": o},
        )

    def gather_copy(par, source, dest, sem):
        piece = g_buf[par].at[pl.ds(source * pb, pb)]
        return pltpu.make_async_remote_copy(
            src_ref=piece,
            dst_ref=piece,
            send_sem=gs_sem.at[par, sem],
            recv_sem=gr_sem.at[par, source],
            device_id={"col": dest},
        )

    def gather_start(par):
        for dz in z_offsets:
            gather_copy(par, j, col_of(dz), dz).start()
        gather_copy(par, j, other, 0).start()

    def gather_wait(par):
        for dz in reversed(z_offsets):
            source = col_of(dz)
            gather_copy(par, source, other, nz + dz).wait_recv()
            gather_copy(par, source, other, nz + dz).start()
        for dz in [0] + z_offsets[::-1]:
            source = lax.rem(z + dz, nz) * 2 + (1 - c)
            gather_copy(par, source, other, dz).wait_recv()

    def gather_done(par):
        for sem in range(2 * nz):
            if sem != nz:
                gather_copy(par, j, other, sem).wait_send()

    def ar_row(n, d):
        index = d[0] * ny + d[1]
        return pltpu.make_async_remote_copy(
            src_ref=st_a.at[n], dst_ref=ar_a.at[n, i],
            send_sem=sa_sem.at[n, index], recv_sem=ra_sem.at[n, index],
            device_id={"row": row_peer(d)},
        )

    def ar_col(n, o):
        return pltpu.make_async_remote_copy(
            src_ref=st_b.at[n], dst_ref=ar_b.at[n, j],
            send_sem=sb_sem.at[n, o], recv_sem=rb_sem.at[n, o],
            device_id={"col": lax.rem(j + o, n_col)},
        )

    def ar_start(n, value):
        st_a[n] = value
        ar_a[n, i] = value
        for d in row_offsets:
            ar_row(n, d).start()

    def ar_middle(n, op):
        for d in reversed(row_offsets):
            ar_row(n, d).wait_recv()
        value = functools.reduce(op, [ar_a[n, s] for s in range(n_row)])
        st_b[n] = value
        ar_b[n, j] = value
        for o in range(1, n_col):
            ar_col(n, o).start()

    def ar_end(n, op):
        for o in range(1, n_col):
            ar_col(n, o).wait_recv()
        value = functools.reduce(op, [ar_b[n, s] for s in range(n_col)])
        for d in row_offsets:
            ar_row(n, d).wait_send()
        for o in range(1, n_col):
            ar_col(n, o).wait_send()
        return value

    def received(par, b):
        at = lax.rem(i, per_half) * pb + b
        parts = [inc_buf[par][within(ctab_s[s, 0, at], slots)] for s in range(n_row)]
        while len(parts) > 1:
            parts = [sum(parts[k : k + 2]) for k in range(0, len(parts), 2)]
        return parts[0]

    def scale_of(total):
        return nodes / jnp.broadcast_to(jnp.sum(total, axis=1, keepdims=True), (K, BLOCK))

    pl.semaphore_wait(barrier, n_row + n_col - 2)

    ar_start(0, seed_sum)
    for d in row_offsets:
        rank_copy(d).start()
    ctab_v[i] = rank_v[i // per_half]
    products(1)
    exchange_start(1)
    ar_middle(0, jnp.add)
    seed_scale = nodes / jnp.broadcast_to(
        jnp.sum(ar_end(0, jnp.add), axis=1, keepdims=True), (K, BLOCK)
    )
    for b in range(pb):
        v = seeds_ref[:, b * BLOCK : (b + 1) * BLOCK].astype(F32) * seed_scale
        v_buf[b] = v
        g_even[j * pb + b] = v.astype(jnp.bfloat16)
    gather_start(0)

    for d in reversed(row_offsets):
        rank_copy(d).wait_recv()
    ctable = pltpu.make_async_copy(ctab_v, ctab_s, tab_sem)
    ctable.start()
    ctable.wait()
    exchange_wait(1)

    def degrees(b, carry):
        deg_buf[b] = received(1, b) + 1.0
        return carry

    lax.fori_loop(0, pb, degrees, 0)
    exchange_done(1)
    for d in row_offsets:
        rank_copy(d).wait_send()

    changes = []
    for it in range(ITERS):
        par = it % 2
        gather_wait(par)
        products(par)
        exchange_start(par)
        gather_done(par)
        exchange_wait(par)

        def advance(b, acc):
            raw = (received(par, b) + v_buf[b]) / deg_buf[b]
            raw_buf[b] = raw
            return acc + raw

        total = lax.fori_loop(0, pb, advance, jnp.zeros((K, BLOCK), F32))
        ar_start(it + 1, total)
        ar_middle(it + 1, jnp.add)
        factor = scale_of(ar_end(it + 1, jnp.add))
        change = jnp.zeros((K, BLOCK), F32)
        for b in range(pb):
            v = raw_buf[b] * factor
            change = jnp.maximum(change, jnp.abs(v - v_buf[b]))
            if it < ITERS - 1:
                v_buf[b] = v
                g_buf[1 - par][j * pb + b] = v.astype(jnp.bfloat16)
            else:
                out_ref[:, b * BLOCK : (b + 1) * BLOCK] = v
        if it < ITERS - 1:
            gather_start(1 - par)
        exchange_done(par)
        changes.append(jnp.max(change, axis=1, keepdims=True))

    sub8 = lax.broadcasted_iota(jnp.int32, (K, BLOCK), 0)
    lane8 = lax.broadcasted_iota(jnp.int32, (K, BLOCK), 1)
    packed = jnp.zeros((K, BLOCK), F32)
    for it in range(ITERS):
        as_row = jnp.sum(jnp.where(sub8 == lane8, changes[it], 0.0), axis=0, keepdims=True)
        packed = jnp.where(sub8 == it, as_row, packed)
    last = ITERS + 1
    ar_start(last, packed)
    ar_middle(last, jnp.maximum)
    most = ar_end(last, jnp.maximum)
    deltas_ref[...] = most[0:ITERS, 0:K]


def solution(mesh, shape=(4, 4, 8)):
    nx, ny, nz = shape

    def on_device(tiles, block_rows, block_cols, counts, seeds):
        n_row, n_col = nx * ny, nz * 2
        tile_total = tiles.shape[2]
        piece = seeds.shape[1]
        pb = piece // BLOCK
        slots = n_row * ROW_CAP
        halves = max(1, n_row * pb // 128)
        nodes = float(piece * n_row * n_col)
        dma = pltpu.SemaphoreType.DMA
        reductions = ITERS + 2
        body = functools.partial(kernel, nx, ny, nz, pb, nodes)
        vmem = pl.BlockSpec(memory_space=pltpu.VMEM)
        return pl.pallas_call(
            body,
            out_shape=(
                jax.ShapeDtypeStruct((K, piece), F32),
                jax.ShapeDtypeStruct((ITERS, K), F32),
            ),
            in_specs=[
                pl.BlockSpec(memory_space=pl.ANY), vmem, vmem,
                pl.BlockSpec(memory_space=pltpu.SMEM), vmem,
            ],
            out_specs=(vmem, vmem),
            scratch_shapes=[
                pltpu.VMEM((tile_total, BLOCK, BLOCK), jnp.bfloat16),
                pltpu.VMEM((n_col * pb, K, BLOCK), jnp.bfloat16),
                pltpu.VMEM((n_col * pb, K, BLOCK), jnp.bfloat16),
                pltpu.VMEM((tile_total + 1, K, BLOCK), F32),
                pltpu.VMEM((2, slots, K, BLOCK), F32),
                pltpu.VMEM((slots + 1, K, BLOCK), F32),
                pltpu.VMEM((slots + 1, K, BLOCK), F32),
                pltpu.VMEM((pb, K, BLOCK), F32),
                pltpu.VMEM((pb, K, BLOCK), F32),
                pltpu.VMEM((pb, K, BLOCK), F32),
                pltpu.VMEM((4, 1, 128), jnp.int32),
                pltpu.SMEM((4, 1, 128), jnp.int32),
                pltpu.VMEM((halves, 1, 128), jnp.int32),
                pltpu.VMEM((n_row, 1, 128), jnp.int32),
                pltpu.SMEM((n_row, 1, 128), jnp.int32),
                pltpu.VMEM((reductions, n_row, K, BLOCK), F32),
                pltpu.VMEM((reductions, n_col, K, BLOCK), F32),
                pltpu.VMEM((reductions, K, BLOCK), F32),
                pltpu.VMEM((reductions, K, BLOCK), F32),
                dma, dma,
                dma((2, n_col)), dma((2, 2 * nz)),
                dma((2, n_row)), dma((2, n_row)),
                dma((n_row,)), dma((n_row,)),
                dma((reductions, n_row)), dma((reductions, n_row)),
                dma((reductions, n_col)), dma((reductions, n_col)),
            ],
            compiler_params=pltpu.CompilerParams(collective_id=0, has_side_effects=True),
        )(tiles, block_rows[0], block_cols[0], counts, seeds)

    return jax.shard_map(
        on_device,
        mesh=mesh,
        in_specs=(
            P("row", "col", None, None, None),
            P("row", "col", None),
            P("row", "col", None),
            P("row", "col"),
            P(None, ("col", "row")),
        ),
        out_specs=(P(None, ("col", "row")), P()),
        check_vma=False,
    )
```

time: 436 us -> 157 us (0.36)
  blocking collectives: 367 us -> 0 us
  Pallas kernels: 0 us -> 153 us
  starting transfers between devices: 23.4 us -> 0 us
  other arithmetic: 19.8 us -> 0 us
  matrix products: 9.01 us -> 0 us
  waiting for transfers between devices: 6.24 us -> 0 us
    psum x20 -> x0, blocking collectives: 194 us -> none  [by_axis(): return functools.reduce(lax.psum, axes, value)]
    pallas_call x0 -> x1, Pallas kernels: none -> 153 us  [on_device(): pl.pallas_call(body, out_shape=(jax.ShapeDtypeStruct((K, piece), F32), ja...]
    all_to_all x3 -> x0, blocking collectives: 75 us -> none  [on_device(): lax.all_to_all(shaped, ROW, split_axis=0, concat_axis=0, tiled=True)]
    all_gather x4 -> x0, blocking collectives: 63.6 us -> none  [on_device(): gathered = lax.all_gather(current_half, COL, axis=0, tiled=True)]
    pmax x4 -> x0, blocking collectives: 34.4 us -> none  [over_axes(): return functools.reduce(lax.pmax, axes, value)]
    all_to_all x2 -> x0, starting transfers between devices: 23.4 us -> none  [the longest x1 15.8 us: in_one_piece(): lax.all_to_all(both, axis, split_axis=split_dim, concat_axis=concat_dim,...]
    dot_general x9 -> x0, matrix products: 9.01 us -> none  [the longest x4 7.43 us: apply_tiles(): jnp.einsum('tkc,trc->tkr', taken_rows, panel_block, preferred_element_typ...]
    scatter-add x5 -> x0, other arithmetic: 7.76 us -> none  [the longest x4 6.65 us: apply_tiles(): return partial_value.at[target_block].add(product * weight[:, None, None])]
  transfers between devices with their start and end apart: 2 -> 0, of which waited for: 1 -> 0; matrix products, arithmetic and copies ran while one was open for 3% -> 0% of each run, Pallas kernels for 0% -> 0%
where the time goes in v1:
time: 157 us
  Pallas kernels  153 us (97%)
  local copies, waits for them, and re-layouts  2.72 us (2%)
    pallas_call x1, Pallas kernels, on_device(): pl.pallas_call(body, out_shape=(jax.ShapeDtypeStruct((K, piece), F32), ja...  153 us

profile of v1, /device:TPU:1, one launch (start us, length us, event | category | flops | bytes accessed | tf_op | source)
XLA Modules:
  0.0 156.8 jit_solution(3209830410251302719)
XLA Ops:
  1.3 152.8 %shard_map.68 = (f32[8,2048]{1,0:T(8,128)}, f32[4,8]{1,0:T(4,128)}) custom-call(bf16[1,1,128,128,128]{4,3,2,1,0:T(8,128)(2,1)} %tiles_ref.1, s32[1,128]{1,0:T(1,128)} %bitcast.2, s32[1,128]{1,0:T(1,128)} %bitcast.3, s32[1,1]{1,0:T(1,128)S(6)} %copy.9.counts_ref, s32[8,2048]{1,0:T(8,128)} %seeds_ref.1), custom_call_target="tpu_custom_call" | custom-call | tf_op jit(solution)/shard_map/pallas_call | solution.py:361
  154.1 1.5 copy.10
  155.5 1.2 copy.11

commit v2 on v1

v2 whole, which is shorter than its diff:
```python
import functools

import jax
import jax.numpy as jnp
from jax import lax
from jax.experimental import pallas as pl
from jax.experimental.pallas import tpu as pltpu
from jax.sharding import PartitionSpec as P

BLOCK = 128
ITERS = 4
ROW_CAP = 4
K = 8
UNROLL = 64
DEAD = 1024
F32 = jnp.float32
BF16 = jnp.bfloat16
I32 = jnp.int32


def within(index, most):
    return jnp.minimum(jnp.maximum(index, 0), most)


def ring(delta, size):
    return min(delta % size, -delta % size)


def split(value):
    high = value.astype(BF16)
    rest = value - high.astype(F32)
    middle = rest.astype(BF16)
    low = (rest - middle.astype(F32)).astype(BF16)
    return high, middle, low


def kernel(
    nx, ny, nz, pb, nodes,
    tiles_ref, rows_ref, cols_ref, counts_ref, seeds_ref,
    out_ref, deltas_ref,
    a_buf, t_buf, g_even, g_odd, s_all, y_buf, p_buf, inc_even, inc_odd, v_buf, raw_buf, w_buf,
    w_row, w_all, ut_buf, u_send, u_in, u_buf,
    tab_v, tab_s, rank_v, ctab_v, ctab_s, ar_a, ar_b, st_a, st_b,
    a_sem, tab_sem, gr_sem, gs_sem, er_sem, es_sem, cr_sem, cs_sem, ra_sem, sa_sem, rb_sem, sb_sem,
    wr_sem, ws_sem, ur_sem, us_sem,
):
    n_row, n_col = nx * ny, nz * 2
    g_buf, inc_buf = (g_even, g_odd, s_all), (inc_even, inc_odd)
    tile_total = a_buf.shape[0]
    slots = n_row * ROW_CAP
    row_blocks, col_blocks = n_row * pb, n_col * pb
    i = lax.axis_index("row")
    j = lax.axis_index("col")
    px, py = i // ny, i % ny
    z, c = j // 2, j % 2
    other = z * 2 + (1 - c)

    row_offsets = sorted(
        [(dx, dy) for dx in range(nx) for dy in range(ny) if (dx, dy) != (0, 0)],
        key=lambda d: -(ring(d[0], nx) + ring(d[1], ny)),
    )

    def row_peer(d):
        return lax.rem(px + d[0], nx) * ny + lax.rem(py + d[1], ny)

    def row_index(d):
        return d[0] * ny + d[1]

    def col_of(dz):
        return lax.rem(z + dz, nz) * 2 + c

    load = pltpu.make_async_copy(tiles_ref.at[0, 0], a_buf, a_sem)
    load.start()

    barrier = pltpu.get_barrier_semaphore()
    for d in row_offsets:
        pl.semaphore_signal(barrier, inc=1, device_id={"row": row_peer(d)})
    for o in range(1, n_col):
        pl.semaphore_signal(barrier, inc=1, device_id={"col": lax.rem(j + o, n_col)})

    def exchange_copy(par, d):
        o = row_peer(d)
        return pltpu.make_async_remote_copy(
            src_ref=p_buf.at[par, pl.ds(o * ROW_CAP, ROW_CAP)],
            dst_ref=inc_buf[par].at[pl.ds(i * ROW_CAP, ROW_CAP)],
            send_sem=es_sem.at[par, row_index(d)],
            recv_sem=er_sem.at[par, row_index(d)],
            device_id={"row": o},
        )

    def exchange_start(par):
        for d in row_offsets:
            exchange_copy(par, d).start()
        inc_buf[par][pl.ds(i * ROW_CAP, ROW_CAP)] = p_buf[par, pl.ds(i * ROW_CAP, ROW_CAP)]

    def exchange_wait(par):
        for d in reversed(row_offsets):
            exchange_copy(par, d).wait_recv()

    def exchange_done(par):
        for d in row_offsets:
            exchange_copy(par, d).wait_send()

    def rank_copy(d):
        o = row_peer(d)
        return pltpu.make_async_remote_copy(
            src_ref=rank_v.at[o // per_half],
            dst_ref=ctab_v.at[i],
            send_sem=cs_sem.at[row_index(d)],
            recv_sem=cr_sem.at[row_index(d)],
            device_id={"row": o},
        )

    def weight_copy(d):
        return pltpu.make_async_remote_copy(
            src_ref=w_row,
            dst_ref=w_all.at[pl.ds(i * pb, pb)],
            send_sem=ws_sem.at[row_index(d)],
            recv_sem=wr_sem.at[row_index(d)],
            device_id={"row": row_peer(d)},
        )

    def u_copy(o):
        dest = lax.rem(j + o, n_col)
        return pltpu.make_async_remote_copy(
            src_ref=u_send.at[pl.ds(dest * pb, pb)],
            dst_ref=u_in.at[j],
            send_sem=us_sem.at[o],
            recv_sem=ur_sem.at[o],
            device_id={"col": dest},
        )

    def gather_copy(par, source, dest, sem):
        piece = g_buf[par].at[pl.ds(source * pb, pb)]
        return pltpu.make_async_remote_copy(
            src_ref=piece,
            dst_ref=piece,
            send_sem=gs_sem.at[par, sem],
            recv_sem=gr_sem.at[par, source],
            device_id={"col": dest},
        )

    two_phase = nz == 8
    direct = [nz - 2, 2, nz - 1, 1] if two_phase else list(range(1, nz))
    sends = 15 if two_phase else 2 * nz - 1

    def gather_start(par):
        for k, dz in enumerate(direct):
            gather_copy(par, j, col_of(dz), k).start()
        gather_copy(par, j, other, len(direct)).start()

    def arrived(par, source):
        gather_copy(par, source, other, 0).wait_recv()

    far = 2 + 4 * (1 - c)

    def gather_middle(par):
        if two_phase:
            arrived(par, col_of(6))
            gather_copy(par, col_of(6), col_of(1), 5).start()
            arrived(par, col_of(2))
            gather_copy(par, col_of(2), col_of(7), 6).start()
            gather_copy(par, col_of(8 - far), col_of(far), 7).start()
            gather_copy(par, col_of(6), other, 8).start()
            gather_copy(par, col_of(2), other, 9).start()

    def gather_wait(par):
        rest = [1, 7, 3, 5, 4] if two_phase else direct
        for k, dz in enumerate(rest):
            arrived(par, col_of(dz))
            gather_copy(par, col_of(dz), other, sends - len(rest) + k).start()
        for dz in [0, 1, nz - 1, 2, nz - 2, 3, nz - 3, 4] if two_phase else range(nz):
            arrived(par, lax.rem(z + dz, nz) * 2 + (1 - c))

    def gather_done(par):
        for sem in range(sends):
            gather_copy(par, j, other, sem).wait_send()

    def ar_row(n, d):
        return pltpu.make_async_remote_copy(
            src_ref=st_a.at[n], dst_ref=ar_a.at[n, i],
            send_sem=sa_sem.at[n, row_index(d)], recv_sem=ra_sem.at[n, row_index(d)],
            device_id={"row": row_peer(d)},
        )

    def ar_col(n, o):
        return pltpu.make_async_remote_copy(
            src_ref=st_b.at[n], dst_ref=ar_b.at[n, j],
            send_sem=sb_sem.at[n, o], recv_sem=rb_sem.at[n, o],
            device_id={"col": lax.rem(j + o, n_col)},
        )

    def tree(op, parts):
        while len(parts) > 1:
            parts = [functools.reduce(op, parts[k : k + 2]) for k in range(0, len(parts), 2)]
        return parts[0]

    def ar_start(n, value):
        st_a[n] = value
        ar_a[n, i] = value
        for d in row_offsets:
            ar_row(n, d).start()

    def ar_middle(n, op):
        for d in reversed(row_offsets):
            ar_row(n, d).wait_recv()
        value = tree(op, [ar_a[n, s] for s in range(n_row)])
        st_b[n] = value
        ar_b[n, j] = value
        for o in range(1, n_col):
            ar_col(n, o).start()

    def ar_end(n, op):
        for o in range(1, n_col):
            ar_col(n, o).wait_recv()
        value = tree(op, [ar_b[n, s] for s in range(n_col)])
        for d in row_offsets:
            ar_row(n, d).wait_send()
        for o in range(1, n_col):
            ar_col(n, o).wait_send()
        return value

    def scale_of(total):
        return nodes / jnp.broadcast_to(jnp.sum(total, axis=1, keepdims=True), (K, BLOCK))

    seed_sum = jnp.zeros((K, BLOCK), F32)
    for b in range(pb):
        seed = seeds_ref[:, b * BLOCK : (b + 1) * BLOCK].astype(F32)
        seed_sum += seed
        s_all[j * pb + b] = seed
    y_buf[tile_total] = jnp.zeros((K, BLOCK), F32)
    for par in range(2):
        inc_buf[par][slots] = jnp.zeros((K, BLOCK), F32)
    w_all[row_blocks : row_blocks + 8] = jnp.zeros((8, BLOCK), F32)

    sub = lax.broadcasted_iota(I32, (tile_total, 128), 0)
    lane = lax.broadcasted_iota(I32, (tile_total, 128), 1)
    count = counts_ref[0, 0]
    lane_row = lax.broadcasted_iota(I32, (1, 128), 1)
    key_r = jnp.where(lane_row < count, rows_ref[0], DEAD)
    key_rr = jnp.broadcast_to(key_r, (tile_total, 128))
    cols_rr = jnp.broadcast_to(cols_ref[0], (tile_total, 128))

    def lanes(value):
        return jnp.sum(value, axis=1, keepdims=True)

    def subs(value):
        return jnp.sum(value, axis=0, keepdims=True)

    def pick_if(mask, value):
        return jnp.where(mask, value, 0)

    key_c = lanes(pick_if(sub == lane, key_rr))
    cols_c = lanes(pick_if(sub == lane, cols_rr))
    key_cc = jnp.broadcast_to(key_c, (tile_total, 128))
    same = key_rr == key_cc
    before = lanes(pick_if(same & (lane < sub), 1))
    pos_c = before + lanes(pick_if(key_rr < key_cc, 1))
    last_c = lanes(pick_if(key_rr <= key_cc, 1)) - 1
    first_c = pick_if((before == 0) & (key_c < DEAD), 1)
    before_r = subs(pick_if(same & (sub < lane), 1))
    first_r = pick_if((before_r == 0) & (key_r < DEAD), 1)
    shift = pb.bit_length() - 1
    owner_c = key_c >> shift
    owner_r = key_r >> shift
    rank_c = lanes(
        pick_if((owner_r == owner_c) & (key_rr < key_cc), jnp.broadcast_to(first_r, sub.shape))
    )
    order = pos_c == lane
    slot_c = owner_c * ROW_CAP + rank_c
    chosen = slot_c == lane
    tab_v[0] = subs(pick_if(order, sub))
    tab_v[1] = subs(pick_if(order, cols_c))
    tab_v[2] = subs(pick_if(order, 1 - first_c))
    tab_v[3] = (
        subs(pick_if(chosen, first_c * last_c)) + (1 - subs(pick_if(chosen, first_c))) * tile_total
    )
    tab_v[4] = jnp.where(lane_row < count, rows_ref[0], row_blocks)
    tab_v[5] = jnp.where(
        subs(pick_if(chosen, first_c)) > 0, subs(pick_if(chosen, first_c * key_c)), row_blocks
    )
    per_half = 128 // pb
    for h in range(rank_v.shape[0]):
        found = subs(pick_if(key_c == lane + 128 * h, first_c * (rank_c + 1)))
        rank_v[h] = jnp.where(found > 0, found - 1 + i * ROW_CAP, slots)
    table = pltpu.make_async_copy(tab_v, tab_s, tab_sem)
    table.start()
    table.wait()
    load.wait()
    ctab_v[i] = rank_v[i // per_half]

    def transpose(at, carry):
        for u in range(8):
            t = at * 8 + u
            t_buf[t] = a_buf[within(tab_s[0, 0, t], tile_total - 1)].T
        return carry

    group = min(8, slots)

    def products(par, ones):
        def step(at, acc):
            for u in range(UNROLL):
                t = at * UNROLL + u
                if ones:
                    x = jnp.ones((K, BLOCK), BF16)
                else:
                    x = g_buf[par][within(tab_s[1, 0, t], col_blocks - 1)]
                y = jnp.dot(x, t_buf[t], preferred_element_type=F32)
                acc = acc * tab_s[2, 0, t].astype(F32) + y
                y_buf[t] = acc
            return acc

        lax.fori_loop(0, tile_total // UNROLL, step, jnp.zeros((K, BLOCK), F32))

        def pick(at, carry):
            for u in range(group):
                q = at * group + u
                p_buf[par, q] = y_buf[within(tab_s[3, 0, q], tile_total)]
            return carry

        lax.fori_loop(0, slots // group, pick, 0)

    def received(par, b):
        at = lax.rem(i, per_half) * pb + b
        return tree(
            jnp.add, [inc_buf[par][within(ctab_s[s, 0, at], slots)] for s in range(n_row)]
        )

    def transposed_products():
        sub8 = lax.broadcasted_iota(I32, (K, BLOCK), 0)

        def step(at, carry):
            for u in range(UNROLL):
                t = at * UNROLL + u
                w = w_all[pl.ds(within(tab_s[4, 0, t], row_blocks), 1), :]
                high, middle, low = (part.astype(F32) for part in split(w))
                rows = jnp.where(sub8 == 0, high, jnp.where(sub8 == 1, middle, low))
                rows = jnp.where(sub8 < 3, rows, 0.0).astype(BF16)
                y = jnp.dot(rows, a_buf[t], preferred_element_type=F32)
                ut_buf[pl.ds(t, 1), :] = jnp.sum(y, axis=0, keepdims=True)
            return carry

        lax.fori_loop(0, tile_total // UNROLL, step, 0)
        block_id = lax.broadcasted_iota(I32, (col_blocks, 128), 0)
        hot = jnp.where(block_id == cols_ref[0], 1.0, 0.0).astype(BF16)
        u_send[...] = sum(
            jnp.dot(hot, part, preferred_element_type=F32) for part in split(ut_buf[...])
        )

    def weighted(q0, carry):
        for u in range(group):
            q = q0 * group + u
            w = w_all[pl.ds(within(tab_s[5, 0, q], row_blocks), 1), :]
            carry += p_buf[0, q] * w
        return carry

    lax.fori_loop(0, tile_total // 8, transpose, 0)
    products(1, True)
    pl.semaphore_wait(barrier, n_row + n_col - 2)
    gather_start(2)
    ar_start(0, seed_sum)
    for d in row_offsets:
        rank_copy(d).start()
    exchange_start(1)
    gather_middle(2)
    ar_middle(0, jnp.add)
    for d in row_offsets:
        rank_copy(d).wait_recv()
    ctable = pltpu.make_async_copy(ctab_v, ctab_s, tab_sem)
    ctable.start()
    ctable.wait()
    exchange_wait(1)

    def degrees(b, carry):
        w = 1.0 / (received(1, b) + 1.0)
        w_buf[b] = w
        w_row[pl.ds(b, 1), :] = w[0:1]
        return carry

    lax.fori_loop(0, pb, degrees, 0)
    for d in row_offsets:
        weight_copy(d).start()
    w_all[pl.ds(i * pb, pb)] = w_row[...]
    gather_wait(2)
    seed_scale = scale_of(ar_end(0, jnp.add))

    def first_half(at, carry):
        for u in range(8):
            g_even[at * 8 + u] = (s_all[at * 8 + u] * seed_scale).astype(BF16)
        return carry

    lax.fori_loop(0, col_blocks // 8, first_half, 0)
    own_total = jnp.zeros((K, BLOCK), F32)
    for b in range(pb):
        v = s_all[j * pb + b] * seed_scale
        v_buf[b] = v
        own_total += v * w_buf[b]
    products(0, False)
    for d in reversed(row_offsets):
        weight_copy(d).wait_recv()
    ar_start(1, lax.fori_loop(0, slots // group, weighted, own_total))
    exchange_start(0)
    transposed_products()
    for o in range(1, n_col):
        u_copy(o).start()
    u_in[j] = u_send[pl.ds(j * pb, pb)]
    ar_middle(1, jnp.add)
    gather_done(2)
    exchange_done(1)
    for d in row_offsets:
        rank_copy(d).wait_send()
    for o in range(1, n_col):
        u_copy(o).wait_recv()
    u_buf[...] = tree(jnp.add, [u_in[s] for s in range(n_col)])

    changes = []
    for it in range(ITERS):
        par = it % 2
        if it > 0:
            gather_middle(par)
            gather_wait(par)
            ar_middle(it + 1, jnp.add)
            products(par, False)
            exchange_start(par)
            gather_done(par)
        exchange_wait(par)
        factor = scale_of(ar_end(it + 1, jnp.add))

        def advance_one(b, carry):
            change, total = carry
            old = v_buf[b]
            v = (received(par, b) + old) * w_buf[b] * factor
            change = jnp.maximum(change, jnp.abs(v - old))
            if it < ITERS - 1:
                v_buf[b] = v
                half = v.astype(BF16)
                g_buf[1 - par][j * pb + b] = half
                total += half.astype(F32) * u_buf[pl.ds(b, 1), :] + v * w_buf[b]
            else:
                raw_buf[b] = v
            return change, total

        def advance(at, carry):
            for u in range(4):
                carry = advance_one(at * 4 + u, carry)
            return carry

        blank = jnp.zeros((K, BLOCK), F32)
        change, total = lax.fori_loop(0, pb // 4, advance, (blank, blank))
        if it < ITERS - 1:
            gather_start(1 - par)
            ar_start(it + 2, total)
        exchange_done(par)
        if it == 0:
            for d in row_offsets:
                weight_copy(d).wait_send()
            for o in range(1, n_col):
                u_copy(o).wait_send()
        changes.append(jnp.max(change, axis=1, keepdims=True))

    sub8 = lax.broadcasted_iota(I32, (K, BLOCK), 0)
    lane8 = lax.broadcasted_iota(I32, (K, BLOCK), 1)
    packed = jnp.zeros((K, BLOCK), F32)
    for it in range(ITERS):
        as_row = jnp.sum(jnp.where(sub8 == lane8, changes[it], 0.0), axis=0, keepdims=True)
        packed = jnp.where(sub8 == it, as_row, packed)
    last = ITERS + 1
    ar_start(last, packed)
    for b in range(pb):
        out_ref[:, b * BLOCK : (b + 1) * BLOCK] = raw_buf[b]
    ar_middle(last, jnp.maximum)
    most = ar_end(last, jnp.maximum)
    deltas_ref[...] = most


def finish(out_in, deltas_in, out_ref, deltas_ref):
    out_ref[...] = out_in[...]
    deltas_ref[...] = deltas_in[0:ITERS, 0:K]


def solution(mesh, shape=(4, 4, 8)):
    nx, ny, nz = shape

    def on_device(tiles, block_rows, block_cols, counts, seeds):
        n_row, n_col = nx * ny, nz * 2
        tile_total = tiles.shape[2]
        piece = seeds.shape[1]
        pb = piece // BLOCK
        slots = n_row * ROW_CAP
        halves = max(1, n_row * pb // 128)
        nodes = float(piece * n_row * n_col)
        dma = pltpu.SemaphoreType.DMA
        reductions = ITERS + 2
        body = functools.partial(kernel, nx, ny, nz, pb, nodes)
        vmem = pl.BlockSpec(memory_space=pltpu.VMEM)
        out, most = pl.pallas_call(
            body,
            out_shape=(
                jax.ShapeDtypeStruct((K, piece), F32),
                jax.ShapeDtypeStruct((K, BLOCK), F32),
            ),
            in_specs=[
                pl.BlockSpec(memory_space=pl.ANY), vmem, vmem,
                pl.BlockSpec(memory_space=pltpu.SMEM), vmem,
            ],
            out_specs=(vmem, vmem),
            scratch_shapes=[
                pltpu.VMEM((tile_total, BLOCK, BLOCK), BF16),
                pltpu.VMEM((tile_total, BLOCK, BLOCK), BF16),
                pltpu.VMEM((n_col * pb, K, BLOCK), BF16),
                pltpu.VMEM((n_col * pb, K, BLOCK), BF16),
                pltpu.VMEM((n_col * pb, K, BLOCK), F32),
                pltpu.VMEM((tile_total + 1, K, BLOCK), F32),
                pltpu.VMEM((2, slots, K, BLOCK), F32),
                pltpu.VMEM((slots + 1, K, BLOCK), F32),
                pltpu.VMEM((slots + 1, K, BLOCK), F32),
                pltpu.VMEM((pb, K, BLOCK), F32),
                pltpu.VMEM((pb, K, BLOCK), F32),
                pltpu.VMEM((pb, K, BLOCK), F32),
                pltpu.VMEM((pb, BLOCK), F32),
                pltpu.VMEM((n_row * pb + 8, BLOCK), F32),
                pltpu.VMEM((tile_total, BLOCK), F32),
                pltpu.VMEM((n_col * pb, BLOCK), F32),
                pltpu.VMEM((n_col, pb, BLOCK), F32),
                pltpu.VMEM((pb, BLOCK), F32),
                pltpu.VMEM((6, 1, 128), I32),
                pltpu.SMEM((6, 1, 128), I32),
                pltpu.VMEM((halves, 1, 128), I32),
                pltpu.VMEM((n_row, 1, 128), I32),
                pltpu.SMEM((n_row, 1, 128), I32),
                pltpu.VMEM((reductions, n_row, K, BLOCK), F32),
                pltpu.VMEM((reductions, n_col, K, BLOCK), F32),
                pltpu.VMEM((reductions, K, BLOCK), F32),
                pltpu.VMEM((reductions, K, BLOCK), F32),
                dma, dma,
                dma((3, n_col)), dma((3, 2 * nz)),
                dma((2, n_row)), dma((2, n_row)),
                dma((n_row,)), dma((n_row,)),
                dma((reductions, n_row)), dma((reductions, n_row)),
                dma((reductions, n_col)), dma((reductions, n_col)),
                dma((n_row,)), dma((n_row,)),
                dma((n_col,)), dma((n_col,)),
            ],
            compiler_params=pltpu.CompilerParams(collective_id=0, has_side_effects=True),
        )(tiles, block_rows[0], block_cols[0], counts, seeds)
        return pl.pallas_call(
            finish,
            out_shape=(
                jax.ShapeDtypeStruct((K, piece), F32),
                jax.ShapeDtypeStruct((ITERS, K), F32),
            ),
            in_specs=[vmem, vmem],
            out_specs=(vmem, vmem),
        )(out, most)

    return jax.shard_map(
        on_device,
        mesh=mesh,
        in_specs=(
            P("row", "col", None, None, None),
            P("row", "col", None),
            P("row", "col", None),
            P("row", "col"),
            P(None, ("col", "row")),
        ),
        out_specs=(P(None, ("col", "row")), P()),
        check_vma=False,
    )
```

time: 157 us -> 111 us (0.71)
  Pallas kernels: 153 us -> 109 us
  local copies, waits for them, and re-layouts: 2.72 us -> 0 us
    pallas_call x1, Pallas kernels: 153 us -> 108 us  [on_device(): pl.pallas_call(body, out_shape=(jax.ShapeDtypeStruct((K, piece), F32), ja...]
    unnamed x2 -> x0, local copies, waits for them, and re-layouts: 2.72 us -> none
where the time goes in v2:
time: 111 us
  Pallas kernels  109 us (98%)
  between operations  1.28 us (1%)
    pallas_call x1, Pallas kernels, on_device(): pl.pallas_call(body, out_shape=(jax.ShapeDtypeStruct((K, piece), F32), ja...  108 us

profile of v2, /device:TPU:1, one launch (start us, length us, event | category | flops | bytes accessed | tf_op | source)
XLA Modules:
  0.0 110.7 jit_solution(18364817199266847920)
XLA Ops:
  1.3 107.9 %shard_map.68 = (f32[8,2048]{1,0:T(8,128)}, f32[8,128]{1,0:T(8,128)}) custom-call(bf16[1,1,128,128,128]{4,3,2,1,0:T(8,128)(2,1)} %tiles_ref.1, s32[1,128]{1,0:T(1,128)} %bitcast.2, s32[1,128]{1,0:T(1,128)} %bitcast.3, s32[1,1]{1,0:T(1,128)S(6)} %copy.7.counts_ref, s32[8,2048]{1,0:T(8,128)} %seeds_ref.1), custom_call_target="tpu_custom_call" | custom-call | tf_op jit(solution)/shard_map/pallas_call | solution.py:496
  109.2 1.5 %shard_map.69 = (f32[8,2048]{1,0:T(8,128)}, f32[4,8]{1,0:T(4,128)}) custom-call(f32[8,2048]{1,0:T(8,128)} %get-tuple-element.4.out_in, f32[8,128]{1,0:T(8,128)} %get-tuple-element.5.deltas_in), custom_call_target="tpu_custom_call" | custom-call | tf_op jit(solution)/shard_map/pallas_call | solution.py:546

commit v3 on v2

--- a/solution.py
+++ b/solution.py
@@ -36,13 +36,14 @@
 
 def kernel(
     nx, ny, nz, pb, nodes,
-    tiles_ref, rows_ref, cols_ref, counts_ref, seeds_ref,
+    tiles_ref, rows_hbm, cols_hbm, counts_hbm, seeds_hbm,
     out_ref, deltas_ref,
+    rows_ref, cols_ref, counts_ref, seeds_ref,
     a_buf, t_buf, g_even, g_odd, s_all, y_buf, p_buf, inc_even, inc_odd, v_buf, raw_buf, w_buf,
-    w_row, w_all, ut_buf, u_send, u_in, u_buf,
+    p_deg, inc_deg, w_row, w_all, ut_buf, u_send, u_in, u_buf,
     tab_v, tab_s, rank_v, ctab_v, ctab_s, ar_a, ar_b, st_a, st_b,
     a_sem, tab_sem, gr_sem, gs_sem, er_sem, es_sem, cr_sem, cs_sem, ra_sem, sa_sem, rb_sem, sb_sem,
-    wr_sem, ws_sem, ur_sem, us_sem,
+    wr_sem, ws_sem, ur_sem, us_sem, in_sem,
 ):
     n_row, n_col = nx * ny, nz * 2
     g_buf, inc_buf = (g_even, g_odd, s_all), (inc_even, inc_odd)
@@ -69,29 +70,47 @@
     def col_of(dz):
         return lax.rem(z + dz, nz) * 2 + c
 
-    load = pltpu.make_async_copy(tiles_ref.at[0, 0], a_buf, a_sem)
-    load.start()
-
+    small = [
+        pltpu.make_async_copy(source, target, in_sem.at[k])
+        for k, (source, target) in enumerate(
+            [
+                (seeds_hbm, seeds_ref),
+                (rows_hbm, rows_ref),
+                (cols_hbm, cols_ref),
+                (counts_hbm, counts_ref),
+            ]
+        )
+    ]
+    for copy in small:
+        copy.start()
     barrier = pltpu.get_barrier_semaphore()
     for d in row_offsets:
         pl.semaphore_signal(barrier, inc=1, device_id={"row": row_peer(d)})
     for o in range(1, n_col):
         pl.semaphore_signal(barrier, inc=1, device_id={"col": lax.rem(j + o, n_col)})
+    load = pltpu.make_async_copy(tiles_ref.at[0, 0], a_buf, a_sem)
+    load.start()
 
     def exchange_copy(par, d):
         o = row_peer(d)
+        there, here = pl.ds(o * ROW_CAP, ROW_CAP), pl.ds(i * ROW_CAP, ROW_CAP)
+        sem = 2 if par is None else par
         return pltpu.make_async_remote_copy(
-            src_ref=p_buf.at[par, pl.ds(o * ROW_CAP, ROW_CAP)],
-            dst_ref=inc_buf[par].at[pl.ds(i * ROW_CAP, ROW_CAP)],
-            send_sem=es_sem.at[par, row_index(d)],
-            recv_sem=er_sem.at[par, row_index(d)],
+            src_ref=p_deg.at[there] if par is None else p_buf.at[par, there],
+            dst_ref=inc_deg.at[here] if par is None else inc_buf[par].at[here],
+            send_sem=es_sem.at[sem, row_index(d)],
+            recv_sem=er_sem.at[sem, row_index(d)],
             device_id={"row": o},
         )
 
     def exchange_start(par):
         for d in row_offsets:
             exchange_copy(par, d).start()
-        inc_buf[par][pl.ds(i * ROW_CAP, ROW_CAP)] = p_buf[par, pl.ds(i * ROW_CAP, ROW_CAP)]
+        here = pl.ds(i * ROW_CAP, ROW_CAP)
+        if par is None:
+            inc_deg[here] = p_deg[here]
+        else:
+            inc_buf[par][here] = p_buf[par, here]
 
     def exchange_wait(par):
         for d in reversed(row_offsets):
@@ -223,23 +242,31 @@
     def scale_of(total):
         return nodes / jnp.broadcast_to(jnp.sum(total, axis=1, keepdims=True), (K, BLOCK))
 
+    y_buf[tile_total] = jnp.zeros((K, BLOCK), F32)
+    for par in range(2):
+        inc_buf[par][slots] = jnp.zeros((K, BLOCK), F32)
+    w_all[row_blocks] = jnp.zeros((1, BLOCK), F32)
+    inc_deg[slots] = jnp.zeros((1, BLOCK), F32)
+    small[0].wait()
     seed_sum = jnp.zeros((K, BLOCK), F32)
     for b in range(pb):
         seed = seeds_ref[:, b * BLOCK : (b + 1) * BLOCK].astype(F32)
         seed_sum += seed
-        s_all[j * pb + b] = seed
-    y_buf[tile_total] = jnp.zeros((K, BLOCK), F32)
-    for par in range(2):
-        inc_buf[par][slots] = jnp.zeros((K, BLOCK), F32)
-    w_all[row_blocks : row_blocks + 8] = jnp.zeros((8, BLOCK), F32)
+        s_all[j * pb + b] = seeds_ref[:, b * BLOCK : (b + 1) * BLOCK].astype(jnp.int16)
+
+    pl.semaphore_wait(barrier, n_row + n_col - 2)
+    gather_start(2)
+    ar_start(0, seed_sum)
+    for copy in small[1:]:
+        copy.wait()
 
     sub = lax.broadcasted_iota(I32, (tile_total, 128), 0)
     lane = lax.broadcasted_iota(I32, (tile_total, 128), 1)
-    count = counts_ref[0, 0]
+    count = counts_ref[...]
     lane_row = lax.broadcasted_iota(I32, (1, 128), 1)
-    key_r = jnp.where(lane_row < count, rows_ref[0], DEAD)
+    key_r = jnp.where(lane_row < count, rows_ref[...], DEAD)
     key_rr = jnp.broadcast_to(key_r, (tile_total, 128))
-    cols_rr = jnp.broadcast_to(cols_ref[0], (tile_total, 128))
+    cols_rr = jnp.broadcast_to(cols_ref[...], (tile_total, 128))
 
     def lanes(value):
         return jnp.sum(value, axis=1, keepdims=True)
@@ -275,7 +302,7 @@
     tab_v[3] = (
         subs(pick_if(chosen, first_c * last_c)) + (1 - subs(pick_if(chosen, first_c))) * tile_total
     )
-    tab_v[4] = jnp.where(lane_row < count, rows_ref[0], row_blocks)
+    tab_v[4] = jnp.where(lane_row < count, rows_ref[...], row_blocks)
     tab_v[5] = jnp.where(
         subs(pick_if(chosen, first_c)) > 0, subs(pick_if(chosen, first_c * key_c)), row_blocks
     )
@@ -289,12 +316,6 @@
     load.wait()
     ctab_v[i] = rank_v[i // per_half]
 
-    def transpose(at, carry):
-        for u in range(8):
-            t = at * 8 + u
-            t_buf[t] = a_buf[within(tab_s[0, 0, t], tile_total - 1)].T
-        return carry
-
     group = min(8, slots)
 
     def products(par, ones):
@@ -303,9 +324,12 @@
                 t = at * UNROLL + u
                 if ones:
                     x = jnp.ones((K, BLOCK), BF16)
+                    tile = a_buf[within(tab_s[0, 0, t], tile_total - 1)].T
+                    t_buf[t] = tile
                 else:
                     x = g_buf[par][within(tab_s[1, 0, t], col_blocks - 1)]
-                y = jnp.dot(x, t_buf[t], preferred_element_type=F32)
+                    tile = t_buf[t]
+                y = jnp.dot(x, tile, preferred_element_type=F32)
                 acc = acc * tab_s[2, 0, t].astype(F32) + y
                 y_buf[t] = acc
             return acc
@@ -315,15 +339,20 @@
         def pick(at, carry):
             for u in range(group):
                 q = at * group + u
-                p_buf[par, q] = y_buf[within(tab_s[3, 0, q], tile_total)]
+                value = y_buf[within(tab_s[3, 0, q], tile_total)]
+                if ones:
+                    p_deg[q] = value[0:1]
+                else:
+                    p_buf[par, q] = value
             return carry
 
         lax.fori_loop(0, slots // group, pick, 0)
 
     def received(par, b):
         at = lax.rem(i, per_half) * pb + b
+        source = inc_deg if par is None else inc_buf[par]
         return tree(
-            jnp.add, [inc_buf[par][within(ctab_s[s, 0, at], slots)] for s in range(n_row)]
+            jnp.add, [source[within(ctab_s[s, 0, at], slots)] for s in range(n_row)]
         )
 
     def transposed_products():
@@ -332,7 +361,7 @@
         def step(at, carry):
             for u in range(UNROLL):
                 t = at * UNROLL + u
-                w = w_all[pl.ds(within(tab_s[4, 0, t], row_blocks), 1), :]
+                w = w_all[within(tab_s[4, 0, t], row_blocks)]
                 high, middle, low = (part.astype(F32) for part in split(w))
                 rows = jnp.where(sub8 == 0, high, jnp.where(sub8 == 1, middle, low))
                 rows = jnp.where(sub8 < 3, rows, 0.0).astype(BF16)
@@ -342,7 +371,7 @@
 
         lax.fori_loop(0, tile_total // UNROLL, step, 0)
         block_id = lax.broadcasted_iota(I32, (col_blocks, 128), 0)
-        hot = jnp.where(block_id == cols_ref[0], 1.0, 0.0).astype(BF16)
+        hot = jnp.where(block_id == cols_ref[...], 1.0, 0.0).astype(BF16)
         u_send[...] = sum(
             jnp.dot(hot, part, preferred_element_type=F32) for part in split(ut_buf[...])
         )
@@ -350,18 +379,14 @@
     def weighted(q0, carry):
         for u in range(group):
             q = q0 * group + u
-            w = w_all[pl.ds(within(tab_s[5, 0, q], row_blocks), 1), :]
+            w = w_all[within(tab_s[5, 0, q], row_blocks)]
             carry += p_buf[0, q] * w
         return carry
 
-    lax.fori_loop(0, tile_total // 8, transpose, 0)
-    products(1, True)
-    pl.semaphore_wait(barrier, n_row + n_col - 2)
-    gather_start(2)
-    ar_start(0, seed_sum)
+    products(None, True)
     for d in row_offsets:
         rank_copy(d).start()
-    exchange_start(1)
+    exchange_start(None)
     gather_middle(2)
     ar_middle(0, jnp.add)
     for d in row_offsets:
@@ -369,15 +394,17 @@
     ctable = pltpu.make_async_copy(ctab_v, ctab_s, tab_sem)
     ctable.start()
     ctable.wait()
-    exchange_wait(1)
-
-    def degrees(b, carry):
-        w = 1.0 / (received(1, b) + 1.0)
-        w_buf[b] = w
-        w_row[pl.ds(b, 1), :] = w[0:1]
+    exchange_wait(None)
+
+    def degrees(at, carry):
+        for u in range(4):
+            b = at * 4 + u
+            w = 1.0 / (received(None, b) + 1.0)
+            w_buf[b] = jnp.broadcast_to(w, (K, BLOCK))
+            w_row[b] = w
         return carry
 
-    lax.fori_loop(0, pb, degrees, 0)
+    lax.fori_loop(0, pb // 4, degrees, 0)
     for d in row_offsets:
         weight_copy(d).start()
     w_all[pl.ds(i * pb, pb)] = w_row[...]
@@ -386,13 +413,13 @@
 
     def first_half(at, carry):
         for u in range(8):
-            g_even[at * 8 + u] = (s_all[at * 8 + u] * seed_scale).astype(BF16)
+            g_even[at * 8 + u] = (s_all[at * 8 + u].astype(I32).astype(F32) * seed_scale).astype(BF16)
         return carry
 
     lax.fori_loop(0, col_blocks // 8, first_half, 0)
     own_total = jnp.zeros((K, BLOCK), F32)
     for b in range(pb):
-        v = s_all[j * pb + b] * seed_scale
+        v = seeds_ref[:, b * BLOCK : (b + 1) * BLOCK].astype(F32) * seed_scale
         v_buf[b] = v
         own_total += v * w_buf[b]
     products(0, False)
@@ -406,12 +433,14 @@
     u_in[j] = u_send[pl.ds(j * pb, pb)]
     ar_middle(1, jnp.add)
     gather_done(2)
-    exchange_done(1)
+    exchange_done(None)
     for d in row_offsets:
         rank_copy(d).wait_send()
     for o in range(1, n_col):
         u_copy(o).wait_recv()
-    u_buf[...] = tree(jnp.add, [u_in[s] for s in range(n_col)])
+    u_sum = tree(jnp.add, [u_in[s] for s in range(n_col)])
+    for b in range(pb):
+        u_buf[b] = u_sum[b : b + 1]
 
     changes = []
     for it in range(ITERS):
@@ -435,7 +464,7 @@
                 v_buf[b] = v
                 half = v.astype(BF16)
                 g_buf[1 - par][j * pb + b] = half
-                total += half.astype(F32) * u_buf[pl.ds(b, 1), :] + v * w_buf[b]
+                total += half.astype(F32) * u_buf[b] + v * w_buf[b]
             else:
                 raw_buf[b] = v
             return change, total
@@ -500,16 +529,19 @@
                 jax.ShapeDtypeStruct((K, BLOCK), F32),
             ),
             in_specs=[
-                pl.BlockSpec(memory_space=pl.ANY), vmem, vmem,
-                pl.BlockSpec(memory_space=pltpu.SMEM), vmem,
+                pl.BlockSpec(memory_space=pltpu.HBM) for _ in range(5)
             ],
             out_specs=(vmem, vmem),
             scratch_shapes=[
+                pltpu.VMEM((1, tile_total), I32),
+                pltpu.VMEM((1, tile_total), I32),
+                pltpu.VMEM((1, 1), I32),
+                pltpu.VMEM((K, piece), I32),
                 pltpu.VMEM((tile_total, BLOCK, BLOCK), BF16),
                 pltpu.VMEM((tile_total, BLOCK, BLOCK), BF16),
                 pltpu.VMEM((n_col * pb, K, BLOCK), BF16),
                 pltpu.VMEM((n_col * pb, K, BLOCK), BF16),
-                pltpu.VMEM((n_col * pb, K, BLOCK), F32),
+                pltpu.VMEM((n_col * pb, K, BLOCK), jnp.int16),
                 pltpu.VMEM((tile_total + 1, K, BLOCK), F32),
                 pltpu.VMEM((2, slots, K, BLOCK), F32),
                 pltpu.VMEM((slots + 1, K, BLOCK), F32),
@@ -517,12 +549,14 @@
                 pltpu.VMEM((pb, K, BLOCK), F32),
                 pltpu.VMEM((pb, K, BLOCK), F32),
                 pltpu.VMEM((pb, K, BLOCK), F32),
-                pltpu.VMEM((pb, BLOCK), F32),
-                pltpu.VMEM((n_row * pb + 8, BLOCK), F32),
+                pltpu.VMEM((slots, 1, BLOCK), F32),
+                pltpu.VMEM((slots + 1, 1, BLOCK), F32),
+                pltpu.VMEM((pb, 1, BLOCK), F32),
+                pltpu.VMEM((n_row * pb + 1, 1, BLOCK), F32),
                 pltpu.VMEM((tile_total, BLOCK), F32),
                 pltpu.VMEM((n_col * pb, BLOCK), F32),
                 pltpu.VMEM((n_col, pb, BLOCK), F32),
-                pltpu.VMEM((pb, BLOCK), F32),
+                pltpu.VMEM((pb, 1, BLOCK), F32),
                 pltpu.VMEM((6, 1, 128), I32),
                 pltpu.SMEM((6, 1, 128), I32),
                 pltpu.VMEM((halves, 1, 128), I32),
@@ -534,12 +568,12 @@
                 pltpu.VMEM((reductions, K, BLOCK), F32),
                 dma, dma,
                 dma((3, n_col)), dma((3, 2 * nz)),
-                dma((2, n_row)), dma((2, n_row)),
+                dma((3, n_row)), dma((3, n_row)),
                 dma((n_row,)), dma((n_row,)),
                 dma((reductions, n_row)), dma((reductions, n_row)),
                 dma((reductions, n_col)), dma((reductions, n_col)),
                 dma((n_row,)), dma((n_row,)),
-                dma((n_col,)), dma((n_col,)),
+                dma((n_col,)), dma((n_col,)), dma((4,)),
             ],
             compiler_params=pltpu.CompilerParams(collective_id=0, has_side_effects=True),
         )(tiles, block_rows[0], block_cols[0], counts, seeds)

time: 111 us -> 106 us (0.955)
  Pallas kernels: 109 us -> 104 us
    pallas_call x1, Pallas kernels: 108 us -> 103 us  [on_device(): pl.pallas_call(body, out_shape=(jax.ShapeDtypeStruct((K, piece), F32), ja...]
where the time goes in v3:
time: 106 us
  Pallas kernels  104 us (98%)
  between operations  1.28 us (1%)
    pallas_call x1, Pallas kernels, on_device(): pl.pallas_call(body, out_shape=(jax.ShapeDtypeStruct((K, piece), F32), ja...  103 us

profile of v3, /device:TPU:1, one launch (start us, length us, event | category | flops | bytes accessed | tf_op | source)
XLA Modules:
  0.0 105.7 jit_solution(10737567267004005511)
XLA Ops:
  1.3 102.9 %shard_map.68 = (f32[8,2048]{1,0:T(8,128)}, f32[8,128]{1,0:T(8,128)}) custom-call(bf16[1,1,128,128,128]{4,3,2,1,0:T(8,128)(2,1)} %tiles_ref.1, s32[1,128]{1,0:T(1,128)} %bitcast.2, s32[1,128]{1,0:T(1,128)} %bitcast.3, s32[1,1]{1,0:T(1,128)S(6)} %copy.7.counts_hbm, s32[8,2048]{1,0:T(8,128)} %seeds_hbm.1), custom_call_target="tpu_custom_call" | custom-call | tf_op jit(solution)/shard_map/pallas_call | solution.py:525
  104.2 1.5 %shard_map.69 = (f32[8,2048]{1,0:T(8,128)}, f32[4,8]{1,0:T(4,128)}) custom-call(f32[8,2048]{1,0:T(8,128)} %get-tuple-element.4.out_in, f32[8,128]{1,0:T(8,128)} %get-tuple-element.5.deltas_in), custom_call_target="tpu_custom_call" | custom-call | tf_op jit(solution)/shard_map/pallas_call | solution.py:580

commit v4 on v3

--- a/solution.py
+++ b/solution.py
@@ -11,7 +11,7 @@
 ITERS = 4
 ROW_CAP = 4
 K = 8
-UNROLL = 64
+UNROLL = 128
 DEAD = 1024
 F32 = jnp.float32
 BF16 = jnp.bfloat16
@@ -312,11 +312,11 @@
         rank_v[h] = jnp.where(found > 0, found - 1 + i * ROW_CAP, slots)
     table = pltpu.make_async_copy(tab_v, tab_s, tab_sem)
     table.start()
+    for d in row_offsets:
+        rank_copy(d).start()
     table.wait()
     load.wait()
     ctab_v[i] = rank_v[i // per_half]
-
-    group = min(8, slots)
 
     def products(par, ones):
         def step(at, acc):
@@ -336,17 +336,12 @@
 
         lax.fori_loop(0, tile_total // UNROLL, step, jnp.zeros((K, BLOCK), F32))
 
-        def pick(at, carry):
-            for u in range(group):
-                q = at * group + u
-                value = y_buf[within(tab_s[3, 0, q], tile_total)]
-                if ones:
-                    p_deg[q] = value[0:1]
-                else:
-                    p_buf[par, q] = value
-            return carry
-
-        lax.fori_loop(0, slots // group, pick, 0)
+        for q in range(slots):
+            value = y_buf[within(tab_s[3, 0, q], tile_total)]
+            if ones:
+                p_deg[q] = value[0:1]
+            else:
+                p_buf[par, q] = value
 
     def received(par, b):
         at = lax.rem(i, per_half) * pb + b
@@ -376,16 +371,14 @@
             jnp.dot(hot, part, preferred_element_type=F32) for part in split(ut_buf[...])
         )
 
-    def weighted(q0, carry):
-        for u in range(group):
-            q = q0 * group + u
+    def weighted(base):
+        sums = [base] + [jnp.zeros((K, BLOCK), F32) for _ in range(3)]
+        for q in range(slots):
             w = w_all[within(tab_s[5, 0, q], row_blocks)]
-            carry += p_buf[0, q] * w
-        return carry
+            sums[q % 4] += p_buf[0, q] * w
+        return tree(jnp.add, sums)
 
     products(None, True)
-    for d in row_offsets:
-        rank_copy(d).start()
     exchange_start(None)
     gather_middle(2)
     ar_middle(0, jnp.add)
@@ -393,18 +386,13 @@
         rank_copy(d).wait_recv()
     ctable = pltpu.make_async_copy(ctab_v, ctab_s, tab_sem)
     ctable.start()
+    exchange_wait(None)
     ctable.wait()
-    exchange_wait(None)
-
-    def degrees(at, carry):
-        for u in range(4):
-            b = at * 4 + u
-            w = 1.0 / (received(None, b) + 1.0)
-            w_buf[b] = jnp.broadcast_to(w, (K, BLOCK))
-            w_row[b] = w
-        return carry
-
-    lax.fori_loop(0, pb // 4, degrees, 0)
+
+    for b in range(pb):
+        w = 1.0 / (received(None, b) + 1.0)
+        w_buf[b] = jnp.broadcast_to(w, (K, BLOCK))
+        w_row[b] = w
     for d in row_offsets:
         weight_copy(d).start()
     w_all[pl.ds(i * pb, pb)] = w_row[...]
@@ -425,7 +413,7 @@
     products(0, False)
     for d in reversed(row_offsets):
         weight_copy(d).wait_recv()
-    ar_start(1, lax.fori_loop(0, slots // group, weighted, own_total))
+    ar_start(1, weighted(own_total))
     exchange_start(0)
     transposed_products()
     for o in range(1, n_col):
@@ -469,13 +457,10 @@
                 raw_buf[b] = v
             return change, total
 
-        def advance(at, carry):
-            for u in range(4):
-                carry = advance_one(at * 4 + u, carry)
-            return carry
-
         blank = jnp.zeros((K, BLOCK), F32)
-        change, total = lax.fori_loop(0, pb // 4, advance, (blank, blank))
+        change, total = blank, blank
+        for b in range(pb):
+            change, total = advance_one(b, (change, total))
         if it < ITERS - 1:
             gather_start(1 - par)
             ar_start(it + 2, total)
@@ -499,12 +484,7 @@
         out_ref[:, b * BLOCK : (b + 1) * BLOCK] = raw_buf[b]
     ar_middle(last, jnp.maximum)
     most = ar_end(last, jnp.maximum)
-    deltas_ref[...] = most
-
-
-def finish(out_in, deltas_in, out_ref, deltas_ref):
-    out_ref[...] = out_in[...]
-    deltas_ref[...] = deltas_in[0:ITERS, 0:K]
+    deltas_ref[...] = most[0:ITERS, 0:K]
 
 
 def solution(mesh, shape=(4, 4, 8)):
@@ -522,11 +502,11 @@
         reductions = ITERS + 2
         body = functools.partial(kernel, nx, ny, nz, pb, nodes)
         vmem = pl.BlockSpec(memory_space=pltpu.VMEM)
-        out, most = pl.pallas_call(
+        return pl.pallas_call(
             body,
             out_shape=(
-                jax.ShapeDtypeStruct((K, piece), F32),
-                jax.ShapeDtypeStruct((K, BLOCK), F32),
+                pltpu.VMEM((K, piece), F32),
+                pltpu.VMEM((ITERS, K), F32),
             ),
             in_specs=[
                 pl.BlockSpec(memory_space=pltpu.HBM) for _ in range(5)
@@ -577,15 +557,6 @@
             ],
             compiler_params=pltpu.CompilerParams(collective_id=0, has_side_effects=True),
         )(tiles, block_rows[0], block_cols[0], counts, seeds)
-        return pl.pallas_call(
-            finish,
-            out_shape=(
-                jax.ShapeDtypeStruct((K, piece), F32),
-                jax.ShapeDtypeStruct((ITERS, K), F32),
-            ),
-            in_specs=[vmem, vmem],
-            out_specs=(vmem, vmem),
-        )(out, most)
 
     return jax.shard_map(
         on_device,

time: 106 us -> 102 us (0.962)
  Pallas kernels: 104 us -> 99.9 us
  local copies, waits for them, and re-layouts: 0 us -> 1.21 us
    pallas_call x2 -> x1, Pallas kernels: 104 us -> 99.9 us  [on_device(): pl.pallas_call(body, out_shape=(pltpu.VMEM((K, piece), F32), pltpu.VMEM((...]
    unnamed x0 -> x2, local copies, waits for them, and re-layouts: none -> 1.21 us
where the time goes in v4:
time: 102 us
  Pallas kernels  99.9 us (98%)
  between operations  1.29 us (1%)
  local copies, waits for them, and re-layouts  1.21 us (1%)
    pallas_call x1, Pallas kernels, on_device(): pl.pallas_call(body, out_shape=(pltpu.VMEM((K, piece), F32), pltpu.VMEM((...  99.9 us

profile of v4, /device:TPU:1, one launch (start us, length us, event | category | flops | bytes accessed | tf_op | source)
XLA Modules:
  0.0 102.4 jit_solution(2910411309872798425)
XLA Ops:
  1.3 99.9 %shard_map.68 = (f32[8,2048]{1,0:T(8,128)S(1)}, f32[4,8]{1,0:T(4,128)S(1)}) custom-call(bf16[1,1,128,128,128]{4,3,2,1,0:T(8,128)(2,1)} %tiles_ref.1, s32[1,128]{1,0:T(1,128)} %bitcast.2, s32[1,128]{1,0:T(1,128)} %bitcast.3, s32[1,1]{1,0:T(1,128)S(6)} %copy.11.counts_hbm, s32[8,2048]{1,0:T(8,128)} %seeds_hbm.1), custom_call_target="tpu_custom_call" | custom-call | tf_op jit(solution)/shard_map/pallas_call | solution.py:505
  101.2 0.6 copy.9
  101.8 0.6 copy.10

commit v5 on v4

--- a/solution.py
+++ b/solution.py
@@ -12,6 +12,7 @@
 ROW_CAP = 4
 K = 8
 UNROLL = 128
+PARTS = 2
 DEAD = 1024
 F32 = jnp.float32
 BF16 = jnp.bfloat16
@@ -149,51 +150,61 @@
             device_id={"col": dest},
         )
 
-    def gather_copy(par, source, dest, sem):
-        piece = g_buf[par].at[pl.ds(source * pb, pb)]
+    cut = pb // PARTS
+
+    def gather_copy(par, source, dest, sem, part):
+        piece = g_buf[par].at[pl.ds(source * pb + part * cut, cut)]
         return pltpu.make_async_remote_copy(
             src_ref=piece,
             dst_ref=piece,
-            send_sem=gs_sem.at[par, sem],
-            recv_sem=gr_sem.at[par, source],
+            send_sem=gs_sem.at[par, sem, part],
+            recv_sem=gr_sem.at[par, source, part],
             device_id={"col": dest},
         )
 
     two_phase = nz == 8
     direct = [nz - 2, 2, nz - 1, 1] if two_phase else list(range(1, nz))
     sends = 15 if two_phase else 2 * nz - 1
-
-    def gather_start(par):
-        for k, dz in enumerate(direct):
-            gather_copy(par, j, col_of(dz), k).start()
-        gather_copy(par, j, other, len(direct)).start()
-
-    def arrived(par, source):
-        gather_copy(par, source, other, 0).wait_recv()
-
     far = 2 + 4 * (1 - c)
+
+    def arrived(par, source, part):
+        gather_copy(par, source, other, 0, part).wait_recv()
+
+    def gather_start(par, part):
+        for k in range(len(direct)):
+            gather_copy(par, j, col_of(direct[k]), k, part).start()
+        gather_copy(par, j, other, len(direct), part).start()
 
     def gather_middle(par):
         if two_phase:
-            arrived(par, col_of(6))
-            gather_copy(par, col_of(6), col_of(1), 5).start()
-            arrived(par, col_of(2))
-            gather_copy(par, col_of(2), col_of(7), 6).start()
-            gather_copy(par, col_of(8 - far), col_of(far), 7).start()
-            gather_copy(par, col_of(6), other, 8).start()
-            gather_copy(par, col_of(2), other, 9).start()
-
-    def gather_wait(par):
+            for part in range(PARTS):
+                arrived(par, col_of(6), part)
+                gather_copy(par, col_of(6), col_of(1), 5, part).start()
+                arrived(par, col_of(2), part)
+                gather_copy(par, col_of(2), col_of(7), 6, part).start()
+                gather_copy(par, col_of(8 - far), col_of(far), 7, part).start()
+                gather_copy(par, col_of(6), other, 8, part).start()
+                gather_copy(par, col_of(2), other, 9, part).start()
+
+    def gather_wait(par, meanwhile=None):
         rest = [1, 7, 3, 5, 4] if two_phase else direct
-        for k, dz in enumerate(rest):
-            arrived(par, col_of(dz))
-            gather_copy(par, col_of(dz), other, sends - len(rest) + k).start()
+        for first in range(0, len(rest), 2):
+            for part in range(PARTS):
+                for k in range(first, min(first + 2, len(rest))):
+                    arrived(par, col_of(rest[k]), part)
+                    gather_copy(
+                        par, col_of(rest[k]), other, sends - len(rest) + k, part
+                    ).start()
+        if meanwhile is not None:
+            meanwhile()
         for dz in [0, 1, nz - 1, 2, nz - 2, 3, nz - 3, 4] if two_phase else range(nz):
-            arrived(par, lax.rem(z + dz, nz) * 2 + (1 - c))
+            for part in range(PARTS):
+                arrived(par, lax.rem(z + dz, nz) * 2 + (1 - c), part)
 
     def gather_done(par):
         for sem in range(sends):
-            gather_copy(par, j, other, sem).wait_send()
+            for part in range(PARTS):
+                gather_copy(par, j, other, sem, part).wait_send()
 
     def ar_row(n, d):
         return pltpu.make_async_remote_copy(
@@ -255,7 +266,8 @@
         s_all[j * pb + b] = seeds_ref[:, b * BLOCK : (b + 1) * BLOCK].astype(jnp.int16)
 
     pl.semaphore_wait(barrier, n_row + n_col - 2)
-    gather_start(2)
+    for part in range(PARTS):
+        gather_start(2, part)
     ar_start(0, seed_sum)
     for copy in small[1:]:
         copy.wait()
@@ -435,34 +447,32 @@
         par = it % 2
         if it > 0:
             gather_middle(par)
-            gather_wait(par)
-            ar_middle(it + 1, jnp.add)
+            gather_wait(par, functools.partial(ar_middle, it + 1, jnp.add))
             products(par, False)
             exchange_start(par)
             gather_done(par)
-        exchange_wait(par)
+        if it == 0:
+            exchange_wait(par)
         factor = scale_of(ar_end(it + 1, jnp.add))
-
-        def advance_one(b, carry):
-            change, total = carry
-            old = v_buf[b]
-            v = (received(par, b) + old) * w_buf[b] * factor
-            change = jnp.maximum(change, jnp.abs(v - old))
+        if it > 0:
+            exchange_wait(par)
+
+        for b in range(pb):
+            v = (received(par, b) + v_buf[b]) * w_buf[b] * factor
+            raw_buf[b] = v
+            if it < ITERS - 1:
+                g_buf[1 - par][j * pb + b] = v.astype(BF16)
+                if (b + 1) % cut == 0:
+                    gather_start(1 - par, b // cut)
+        change = jnp.zeros((K, BLOCK), F32)
+        total = jnp.zeros((K, BLOCK), F32)
+        for b in range(pb):
+            v = raw_buf[b]
+            change = jnp.maximum(change, jnp.abs(v - v_buf[b]))
             if it < ITERS - 1:
                 v_buf[b] = v
-                half = v.astype(BF16)
-                g_buf[1 - par][j * pb + b] = half
-                total += half.astype(F32) * u_buf[b] + v * w_buf[b]
-            else:
-                raw_buf[b] = v
-            return change, total
-
-        blank = jnp.zeros((K, BLOCK), F32)
-        change, total = blank, blank
-        for b in range(pb):
-            change, total = advance_one(b, (change, total))
+                total += v.astype(BF16).astype(F32) * u_buf[b] + v * w_buf[b]
         if it < ITERS - 1:
-            gather_start(1 - par)
             ar_start(it + 2, total)
         exchange_done(par)
         if it == 0:
@@ -547,7 +557,7 @@
                 pltpu.VMEM((reductions, K, BLOCK), F32),
                 pltpu.VMEM((reductions, K, BLOCK), F32),
                 dma, dma,
-                dma((3, n_col)), dma((3, 2 * nz)),
+                dma((3, n_col, PARTS)), dma((3, 2 * nz, PARTS)),
                 dma((3, n_row)), dma((3, n_row)),
                 dma((n_row,)), dma((n_row,)),
                 dma((reductions, n_row)), dma((reductions, n_row)),

time: 102 us -> 102 us (level)
  no operation moved by 1% of the time
where the time goes in v5:
time: 102 us
  Pallas kernels  99.1 us (97%)
  between operations  1.29 us (1%)
  local copies, waits for them, and re-layouts  1.21 us (1%)
    pallas_call x1, Pallas kernels, on_device(): pl.pallas_call(body, out_shape=(pltpu.VMEM((K, piece), F32), pltpu.VMEM((...  99.1 us

profile of v5, /device:TPU:1, one launch (start us, length us, event | category | flops | bytes accessed | tf_op | source)
XLA Modules:
  0.0 101.6 jit_solution(8398101734959271545)
XLA Ops:
  1.3 99.1 %shard_map.68 = (f32[8,2048]{1,0:T(8,128)S(1)}, f32[4,8]{1,0:T(4,128)S(1)}) custom-call(bf16[1,1,128,128,128]{4,3,2,1,0:T(8,128)(2,1)} %tiles_ref.1, s32[1,128]{1,0:T(1,128)} %bitcast.2, s32[1,128]{1,0:T(1,128)} %bitcast.3, s32[1,1]{1,0:T(1,128)S(6)} %copy.11.counts_hbm, s32[8,2048]{1,0:T(8,128)} %seeds_hbm.1), custom_call_target="tpu_custom_call" | custom-call | tf_op jit(solution)/shard_map/pallas_call | solution.py:515
  100.4 0.6 copy.9
  101.1 0.6 copy.10

commit v6 on v5

--- a/solution.py
+++ b/solution.py
@@ -408,25 +408,25 @@
     for d in row_offsets:
         weight_copy(d).start()
     w_all[pl.ds(i * pb, pb)] = w_row[...]
+    own_total = jnp.zeros((K, BLOCK), F32)
+    for b in range(pb):
+        own_total += seeds_ref[:, b * BLOCK : (b + 1) * BLOCK].astype(F32) * w_buf[b]
     gather_wait(2)
     seed_scale = scale_of(ar_end(0, jnp.add))
 
     def first_half(at, carry):
-        for u in range(8):
-            g_even[at * 8 + u] = (s_all[at * 8 + u].astype(I32).astype(F32) * seed_scale).astype(BF16)
+        for u in range(32):
+            g_even[at * 32 + u] = (s_all[at * 32 + u].astype(I32).astype(F32) * seed_scale).astype(BF16)
         return carry
 
-    lax.fori_loop(0, col_blocks // 8, first_half, 0)
-    own_total = jnp.zeros((K, BLOCK), F32)
-    for b in range(pb):
-        v = seeds_ref[:, b * BLOCK : (b + 1) * BLOCK].astype(F32) * seed_scale
-        v_buf[b] = v
-        own_total += v * w_buf[b]
+    lax.fori_loop(0, col_blocks // 32, first_half, 0)
     products(0, False)
     for d in reversed(row_offsets):
         weight_copy(d).wait_recv()
-    ar_start(1, weighted(own_total))
+    ar_start(1, weighted(own_total * seed_scale))
     exchange_start(0)
+    for b in range(pb):
+        v_buf[b] = seeds_ref[:, b * BLOCK : (b + 1) * BLOCK].astype(F32) * seed_scale
     transposed_products()
     for o in range(1, n_col):
         u_copy(o).start()

time: 102 us -> 102 us (level)
  no operation moved by 1% of the time
where the time goes in v6:
time: 102 us; the launch traced here: 101 us
  Pallas kernels  99 us (97%)
  between operations  1.29 us (1%)
  local copies, waits for them, and re-layouts  1.21 us (1%)
    pallas_call x1, Pallas kernels, on_device(): pl.pallas_call(body, out_shape=(pltpu.VMEM((K, piece), F32), pltpu.VMEM((...  99 us

profile of v6, /device:TPU:1, one launch (start us, length us, event | category | flops | bytes accessed | tf_op | source)
XLA Modules:
  0.0 101.5 jit_solution(5634452468027444466)
XLA Ops:
  1.3 99.0 %shard_map.68 = (f32[8,2048]{1,0:T(8,128)S(1)}, f32[4,8]{1,0:T(4,128)S(1)}) custom-call(bf16[1,1,128,128,128]{4,3,2,1,0:T(8,128)(2,1)} %tiles_ref.1, s32[1,128]{1,0:T(1,128)} %bitcast.2, s32[1,128]{1,0:T(1,128)} %bitcast.3, s32[1,1]{1,0:T(1,128)S(6)} %copy.11.counts_hbm, s32[8,2048]{1,0:T(8,128)} %seeds_hbm.1), custom_call_target="tpu_custom_call" | custom-call | tf_op jit(solution)/shard_map/pallas_call | solution.py:515
  100.3 0.6 copy.9
  100.9 0.6 copy.10
